TPU v7x, 16 devices: a whole 2x2x2 slice. The times are simulated.
16 devices in a mesh: replica: 2 (over z), data: 8 (over y, x, core).
Axes of the slice: x: 2, y: 2, z: 2, core: 2. Of those that a mesh axis runs over, the one named last changes fastest.
Arguments:
- img_x: bfloat16 [32768, 640], P(('replica', 'data'))
- txt_x: bfloat16 [32768, 768], P(('replica', 'data'))
- w_img: bfloat16 [640, 640], replicated
- w_txt: bfloat16 [768, 640], replicated
- log_temp: float32 [1], replicated
- logit_bias: float32 [1], replicated
Outputs:
- output 1: float32 [1], replicated
- output 2: float32 [1], replicated
- output 3: float32 [1], replicated
- output 4: float32 [640, 640], replicated
- output 5: float32 [768, 640], replicated
All inputs are finite; a program needn't handle non-finite values.
Results may differ from a plain program's by a relative error of at most 0.001.
Values are sent between devices in bfloat16 or wider.
A program may use at most 1 GiB of HBM per device.

v0:
```python
import jax
import jax.numpy as jnp
from jax import lax
from jax.sharding import PartitionSpec as P


def normalize(raw):
    return raw * lax.rsqrt(jnp.sum(raw * raw, axis=-1, keepdims=True))


def embed_rows(feat_x, w_proj):
    raw_emb = jnp.dot(feat_x, w_proj, preferred_element_type=jnp.float32)
    unit_emb, pull_back = jax.vjp(normalize, raw_emb)
    return unit_emb.astype(jnp.bfloat16), pull_back


def tile_terms(img_emb, txt_blk, labels, temp_scale, bias_val, total_rows):
    sim_tile = jnp.einsum("id,jd->ij", img_emb, txt_blk, preferred_element_type=jnp.float32)
    logits = temp_scale * sim_tile + bias_val
    loss_part = -jnp.sum(jax.nn.log_sigmoid(labels * logits))
    grad_tile = -labels * jax.nn.sigmoid(-labels * logits) / total_rows
    grad_b = grad_tile.astype(jnp.bfloat16)
    d_img = jnp.dot(grad_b, txt_blk, preferred_element_type=jnp.float32)
    d_txt = jnp.einsum("ij,id->jd", grad_b, img_emb, preferred_element_type=jnp.float32)
    return loss_part, jnp.sum(grad_tile * sim_tile), jnp.sum(grad_tile), d_img, d_txt


def solution(mesh):
    rep_count = mesh.shape["replica"]
    data_count = mesh.shape["data"]
    dev_count = rep_count * data_count
    batch_axes = ("replica", "data")
    next_perm = [(k, (k + 1) % dev_count) for k in range(dev_count)]

    def local_fn(img_x, txt_x, w_img, w_txt, log_temp, logit_bias):
        local_rows = img_x.shape[0]
        total_rows = local_rows * dev_count
        img_emb, img_pull = embed_rows(img_x, w_img)
        txt_emb, txt_pull = embed_rows(txt_x, w_txt)
        temp_scale = jnp.exp(log_temp[0])
        bias_val = logit_bias[0]
        row_ids = lax.broadcasted_iota(jnp.int32, (local_rows, 1), 0)
        col_ids = lax.broadcasted_iota(jnp.int32, (1, local_rows), 1)
        diag_labels = jnp.where(row_ids == col_ids, 1.0, -1.0)
        first = tile_terms(img_emb, txt_emb, diag_labels, temp_scale, bias_val, total_rows)

        def hop(step, state):
            txt_blk, d_txt_acc, d_img_acc, loss_acc, temp_acc, bias_acc = state
            txt_blk = lax.ppermute(txt_blk, batch_axes, next_perm)
            d_txt_acc = lax.ppermute(d_txt_acc, batch_axes, next_perm)
            loss_part, temp_part, bias_part, d_img_part, d_txt_part = tile_terms(img_emb, txt_blk, -1.0, temp_scale, bias_val, total_rows)
            return (txt_blk, d_txt_acc + d_txt_part, d_img_acc + d_img_part, loss_acc + loss_part, temp_acc + temp_part, bias_acc + bias_part)

        init_state = (txt_emb, first[4], first[3], first[0], first[1], first[2])
        final_state = lax.fori_loop(1, dev_count, hop, init_state)
        d_txt_home = lax.ppermute(final_state[1], batch_axes, next_perm)
        d_img_raw = img_pull(temp_scale * final_state[2])[0].astype(jnp.bfloat16)
        d_txt_raw = txt_pull(temp_scale * d_txt_home)[0].astype(jnp.bfloat16)
        d_w_img = jnp.einsum("nf,nd->fd", img_x, d_img_raw, preferred_element_type=jnp.float32)
        d_w_txt = jnp.einsum("nf,nd->fd", txt_x, d_txt_raw, preferred_element_type=jnp.float32)
        loss_total, temp_total, bias_total, d_w_img, d_w_txt = lax.psum((final_state[3], final_state[4], final_state[5], d_w_img, d_w_txt), batch_axes)
        loss_out = jnp.reshape(loss_total / total_rows, (1,))
        d_log_temp = jnp.reshape(temp_scale * temp_total, (1,))
        d_logit_bias = jnp.reshape(bias_total, (1,))
        return loss_out, d_log_temp, d_logit_bias, d_w_img, d_w_txt

    batch_spec = P(batch_axes, None)
    return jax.shard_map(local_fn, mesh=mesh, in_specs=(batch_spec, batch_spec, P(), P(), P(), P()), out_specs=(P(), P(), P(), P(), P()), check_vma=False)
```

profile of v0, /device:TPU:0, one launch (start us, length us, event | category | flops | bytes accessed | tf_op | source)
XLA Modules:
  0.0 1781.2 jit_solution(2284455734491025609)
XLA Ops:
  17.1 28.4 %fusion.43 = (f32[]{:T(128)}, f32[]{:T(128)}, f32[]{:T(128)}, bf16[2048,2048]{1,0:T(8,128)(2,1)S(1)}) fusion(f32[]{:T(128)} %bitcast.33, f32[]{:T(128)} %bitcast, bf16[2048,640]{0,1:T(8,128)(2,1)S(1)} %multiply_convert_fusion, bf16[2048,640]{0,1:T(8,128)(2,1)S(1)} %multiply_convert_fusion.1), kind=kOutput, calls=%fused_computation.53 | convolution fusion | flops 5469372416 | bytes 13631508 | tf_op jit(solution)/shard_map/id,jd->ij/dot_general | solution.py:18
  71.2 1528.0 %while.20 = (s32[]{:T(128)}, bf16[2048,640]{1,0:T(8,128)(2,1)}, f32[2048,640]{1,0:T(8,128)}, f32[2048,640]{1,0:T(8,128)}, f32[]{:T(128)}, /*index=5*/f32[]{:T(12...) while((s32[]{:T(128)}, bf16[2048,640]{1,0:T(8,128)(2,1)}, ...), condition=%wide.region_9.10_spmd, body=%wide.region_5.9_spmd.sunk | while | flops 16242966528 | bytes 179306896 | solution.py:55
  74.8 30.6 %collective-permute-done = bf16[2048,640]{1,0:T(8,128)(2,1)} collective-permute-done((bf16[2048,640]{1,0:T(8,128)(2,1)}, bf16[2048,640]{1,0:T(8,128)(2,1)}, u32[]{:S(2)}, u32[]{:S(2)}) %collective-permute-start) | collective-permute-done | bytes 2621472 | tf_op jit(solution)/shard_map/while/body/eval_jaxpr/ppermute | solution.py:49
  174.8 32.4 %collective-permute-done = bf16[2048,640]{1,0:T(8,128)(2,1)} collective-permute-done((bf16[2048,640]{1,0:T(8,128)(2,1)}, bf16[2048,640]{1,0:T(8,128)(2,1)}, u32[]{:S(2)}, u32[]{:S(2)}) %collective-permute-start) | collective-permute-done | bytes 2621472 | tf_op jit(solution)/shard_map/while/body/eval_jaxpr/ppermute | solution.py:49
  207.2 26.3 %fusion.76 = (f32[]{:T(128)}, f32[]{:T(128)}, f32[]{:T(128)}, f32[2048,2048]{1,0:T(8,128)}) fusion(f32[]{:T(128)} %get-tuple-element.224, f32[]{:T(128)} %get-tuple-element.222, bf16[2048,640]{1,0:T(8,128)(2,1)} %get-tuple-element.223, bf16[2048,640]{1,0:T(8,128)(2,1)} %collective-permute-done), kind=kOutput, calls=%fused_computation.11.clone.1 | convolution fusion | flops 5444206592 | bytes 22020116 | tf_op jit(solution)/shard_map/while/body/eval_jaxpr/id,jd->ij/dot_general | solution.py:18
  276.1 32.9 %collective-permute-done = bf16[2048,640]{1,0:T(8,128)(2,1)} collective-permute-done((bf16[2048,640]{1,0:T(8,128)(2,1)}, bf16[2048,640]{1,0:T(8,128)(2,1)}, u32[]{:S(2)}, u32[]{:S(2)}) %collective-permute-start) | collective-permute-done | bytes 2621472 | tf_op jit(solution)/shard_map/while/body/eval_jaxpr/ppermute | solution.py:49
  377.9 32.9 %collective-permute-done = bf16[2048,640]{1,0:T(8,128)(2,1)} collective-permute-done((bf16[2048,640]{1,0:T(8,128)(2,1)}, bf16[2048,640]{1,0:T(8,128)(2,1)}, u32[]{:S(2)}, u32[]{:S(2)}) %collective-permute-start) | collective-permute-done | bytes 2621472 | tf_op jit(solution)/shard_map/while/body/eval_jaxpr/ppermute | solution.py:49
  479.6 32.9 %collective-permute-done = bf16[2048,640]{1,0:T(8,128)(2,1)} collective-permute-done((bf16[2048,640]{1,0:T(8,128)(2,1)}, bf16[2048,640]{1,0:T(8,128)(2,1)}, u32[]{:S(2)}, u32[]{:S(2)}) %collective-permute-start) | collective-permute-done | bytes 2621472 | tf_op jit(solution)/shard_map/while/body/eval_jaxpr/ppermute | solution.py:49
  512.5 26.3 %fusion.76 = (f32[]{:T(128)}, f32[]{:T(128)}, f32[]{:T(128)}, f32[2048,2048]{1,0:T(8,128)}) fusion(f32[]{:T(128)} %get-tuple-element.224, f32[]{:T(128)} %get-tuple-element.222, bf16[2048,640]{1,0:T(8,128)(2,1)} %get-tuple-element.223, bf16[2048,640]{1,0:T(8,128)(2,1)} %collective-permute-done), kind=kOutput, calls=%fused_computation.11.clone.1 | convolution fusion | flops 5444206592 | bytes 22020116 | tf_op jit(solution)/shard_map/while/body/eval_jaxpr/id,jd->ij/dot_general | solution.py:18
  581.4 32.9 %collective-permute-done = bf16[2048,640]{1,0:T(8,128)(2,1)} collective-permute-done((bf16[2048,640]{1,0:T(8,128)(2,1)}, bf16[2048,640]{1,0:T(8,128)(2,1)}, u32[]{:S(2)}, u32[]{:S(2)}) %collective-permute-start) | collective-permute-done | bytes 2621472 | tf_op jit(solution)/shard_map/while/body/eval_jaxpr/ppermute | solution.py:49
  683.1 32.9 %collective-permute-done = bf16[2048,640]{1,0:T(8,128)(2,1)} collective-permute-done((bf16[2048,640]{1,0:T(8,128)(2,1)}, bf16[2048,640]{1,0:T(8,128)(2,1)}, u32[]{:S(2)}, u32[]{:S(2)}) %collective-permute-start) | collective-permute-done | bytes 2621472 | tf_op jit(solution)/shard_map/while/body/eval_jaxpr/ppermute | solution.py:49
  784.9 32.9 %collective-permute-done = bf16[2048,640]{1,0:T(8,128)(2,1)} collective-permute-done((bf16[2048,640]{1,0:T(8,128)(2,1)}, bf16[2048,640]{1,0:T(8,128)(2,1)}, u32[]{:S(2)}, u32[]{:S(2)}) %collective-permute-start) | collective-permute-done | bytes 2621472 | tf_op jit(solution)/shard_map/while/body/eval_jaxpr/ppermute | solution.py:49
  886.7 32.9 %collective-permute-done = bf16[2048,640]{1,0:T(8,128)(2,1)} collective-permute-done((bf16[2048,640]{1,0:T(8,128)(2,1)}, bf16[2048,640]{1,0:T(8,128)(2,1)}, u32[]{:S(2)}, u32[]{:S(2)}) %collective-permute-start) | collective-permute-done | bytes 2621472 | tf_op jit(solution)/shard_map/while/body/eval_jaxpr/ppermute | solution.py:49
  919.5 26.3 %fusion.76 = (f32[]{:T(128)}, f32[]{:T(128)}, f32[]{:T(128)}, f32[2048,2048]{1,0:T(8,128)}) fusion(f32[]{:T(128)} %get-tuple-element.224, f32[]{:T(128)} %get-tuple-element.222, bf16[2048,640]{1,0:T(8,128)(2,1)} %get-tuple-element.223, bf16[2048,640]{1,0:T(8,128)(2,1)} %collective-permute-done), kind=kOutput, calls=%fused_computation.11.clone.1 | convolution fusion | flops 5444206592 | bytes 22020116 | tf_op jit(solution)/shard_map/while/body/eval_jaxpr/id,jd->ij/dot_general | solution.py:18
  988.4 32.9 %collective-permute-done = bf16[2048,640]{1,0:T(8,128)(2,1)} collective-permute-done((bf16[2048,640]{1,0:T(8,128)(2,1)}, bf16[2048,640]{1,0:T(8,128)(2,1)}, u32[]{:S(2)}, u32[]{:S(2)}) %collective-permute-start) | collective-permute-done | bytes 2621472 | tf_op jit(solution)/shard_map/while/body/eval_jaxpr/ppermute | solution.py:49
  1090.2 32.9 %collective-permute-done = bf16[2048,640]{1,0:T(8,128)(2,1)} collective-permute-done((bf16[2048,640]{1,0:T(8,128)(2,1)}, bf16[2048,640]{1,0:T(8,128)(2,1)}, u32[]{:S(2)}, u32[]{:S(2)}) %collective-permute-start) | collective-permute-done | bytes 2621472 | tf_op jit(solution)/shard_map/while/body/eval_jaxpr/ppermute | solution.py:49
  1192.0 32.9 %collective-permute-done = bf16[2048,640]{1,0:T(8,128)(2,1)} collective-permute-done((bf16[2048,640]{1,0:T(8,128)(2,1)}, bf16[2048,640]{1,0:T(8,128)(2,1)}, u32[]{:S(2)}, u32[]{:S(2)}) %collective-permute-start) | collective-permute-done | bytes 2621472 | tf_op jit(solution)/shard_map/while/body/eval_jaxpr/ppermute | solution.py:49
  1293.7 32.9 %collective-permute-done = bf16[2048,640]{1,0:T(8,128)(2,1)} collective-permute-done((bf16[2048,640]{1,0:T(8,128)(2,1)}, bf16[2048,640]{1,0:T(8,128)(2,1)}, u32[]{:S(2)}, u32[]{:S(2)}) %collective-permute-start) | collective-permute-done | bytes 2621472 | tf_op jit(solution)/shard_map/while/body/eval_jaxpr/ppermute | solution.py:49
  1326.6 26.3 %fusion.76 = (f32[]{:T(128)}, f32[]{:T(128)}, f32[]{:T(128)}, f32[2048,2048]{1,0:T(8,128)}) fusion(f32[]{:T(128)} %get-tuple-element.224, f32[]{:T(128)} %get-tuple-element.222, bf16[2048,640]{1,0:T(8,128)(2,1)} %get-tuple-element.223, bf16[2048,640]{1,0:T(8,128)(2,1)} %collective-permute-done), kind=kOutput, calls=%fused_computation.11.clone.1 | convolution fusion | flops 5444206592 | bytes 22020116 | tf_op jit(solution)/shard_map/while/body/eval_jaxpr/id,jd->ij/dot_general | solution.py:18
  1395.5 32.9 %collective-permute-done = bf16[2048,640]{1,0:T(8,128)(2,1)} collective-permute-done((bf16[2048,640]{1,0:T(8,128)(2,1)}, bf16[2048,640]{1,0:T(8,128)(2,1)}, u32[]{:S(2)}, u32[]{:S(2)}) %collective-permute-start) | collective-permute-done | bytes 2621472 | tf_op jit(solution)/shard_map/while/body/eval_jaxpr/ppermute | solution.py:49
  1497.2 32.9 %collective-permute-done = bf16[2048,640]{1,0:T(8,128)(2,1)} collective-permute-done((bf16[2048,640]{1,0:T(8,128)(2,1)}, bf16[2048,640]{1,0:T(8,128)(2,1)}, u32[]{:S(2)}, u32[]{:S(2)}) %collective-permute-start) | collective-permute-done | bytes 2621472 | tf_op jit(solution)/shard_map/while/body/eval_jaxpr/ppermute | solution.py:49
  1611.1 55.0 %collective-permute-done.2 = f32[2048,640]{0,1:T(8,128)} collective-permute-done((f32[2048,640]{0,1:T(8,128)}, f32[2048,640]{0,1:T(8,128)}, u32[]{:S(2)}, u32[]{:S(2)}) %collective-permute-start.2) | collective-permute-done | bytes 5242912 | tf_op jit(solution)/shard_map/ppermute | solution.py:56
  1689.6 33.2 %all-reduce = (f32[]{:T(128)}, f32[]{:T(128)}, f32[1]{0:T(128)}) all-reduce(f32[]{:T(128)} %get-tuple-element.61, f32[]{:T(128)} %get-tuple-element.62, f32[1]{0:T(128)} %bitcast.4), channel_id=1, replica_groups=mesh['replica'=2,'data'=8] {'replica','data'}, use_global_device_ids=true, to_apply=%region_10.11 | all-reduce | flops 3 | bytes 24 | tf_op jit(solution)/shard_map/psum | solution.py:61
  1724.0 42.0 %all-reduce.4.cloned.1.call-done = (f32[640,640]{0,1:T(8,128)}, f32[768,640]{0,1:T(8,128)}) async-done(((f32[640,640]{0,1:T(8,128)}, f32[768,640]{0,1:T(8,128)}), (f32[640,640]{0,1:T(8,128)}, f32[768,640]{0,1:T(8,128)})) %all-reduce.4.cloned.1.call-update) | async-done | bytes 3604496 | tf_op jit(solution)/shard_map/psum | solution.py:61
  (323 shorter events, 929.6 us)
Async XLA Ops:
  7.2 1758.9 %all-reduce.4.cloned.1.call-start = ((), (), s32[]{:S(2)}) async-start(), calls=%async_computation | async-start | bytes 7208960 | tf_op jit(solution)/shard_map/psum | solution.py:61
  71.4 34.0 %collective-permute-start = (bf16[2048,640]{1,0:T(8,128)(2,1)}, bf16[2048,640]{1,0:T(8,128)(2,1)}, u32[]{:S(2)}, u32[]{:S(2)}) collective-permute-start(bf16[2048,640]{1,0:T(8,128)(2,1)} %get-tuple-element.205), channel_id=1, source_target_pairs={{0,1},{1,2},{2,3},{3,4},{4,5},{5,6},{6,7},{7,8},{8,9},{9,10},{10,1... | collective-permute-start | bytes 7864328 | tf_op jit(solution)/shard_map/while/body/eval_jaxpr/ppermute | solution.py:49
  72.2 89.4 %collective-permute-start.1 = (f32[2048,640]{1,0:T(8,128)}, f32[2048,640]{1,0:T(8,128)}, u32[]{:S(2)}, u32[]{:S(2)}) collective-permute-start(f32[2048,640]{1,0:T(8,128)} %get-tuple-element.206), channel_id=1, source_target_pairs={{0,1},{1,2},{2,3},{3,4},{4,5},{5,6},{6,7},{7,8},{8,9},{9,10},{10,1... | collective-permute-start | bytes 15728648 | tf_op jit(solution)/shard_map/while/body/eval_jaxpr/ppermute | solution.py:50
  174.3 32.9 %collective-permute-start = (bf16[2048,640]{1,0:T(8,128)(2,1)}, bf16[2048,640]{1,0:T(8,128)(2,1)}, u32[]{:S(2)}, u32[]{:S(2)}) collective-permute-start(bf16[2048,640]{1,0:T(8,128)(2,1)} %get-tuple-element.205), channel_id=1, source_target_pairs={{0,1},{1,2},{2,3},{3,4},{4,5},{5,6},{6,7},{7,8},{8,9},{9,10},{10,1... | collective-permute-start | bytes 7864328 | tf_op jit(solution)/shard_map/while/body/eval_jaxpr/ppermute | solution.py:49
  174.3 89.0 %collective-permute-start.1 = (f32[2048,640]{1,0:T(8,128)}, f32[2048,640]{1,0:T(8,128)}, u32[]{:S(2)}, u32[]{:S(2)}) collective-permute-start(f32[2048,640]{1,0:T(8,128)} %get-tuple-element.206), channel_id=1, source_target_pairs={{0,1},{1,2},{2,3},{3,4},{4,5},{5,6},{6,7},{7,8},{8,9},{9,10},{10,1... | collective-permute-start | bytes 15728648 | tf_op jit(solution)/shard_map/while/body/eval_jaxpr/ppermute | solution.py:50
  276.1 32.9 %collective-permute-start = (bf16[2048,640]{1,0:T(8,128)(2,1)}, bf16[2048,640]{1,0:T(8,128)(2,1)}, u32[]{:S(2)}, u32[]{:S(2)}) collective-permute-start(bf16[2048,640]{1,0:T(8,128)(2,1)} %get-tuple-element.205), channel_id=1, source_target_pairs={{0,1},{1,2},{2,3},{3,4},{4,5},{5,6},{6,7},{7,8},{8,9},{9,10},{10,1... | collective-permute-start | bytes 7864328 | tf_op jit(solution)/shard_map/while/body/eval_jaxpr/ppermute | solution.py:49
  276.1 89.0 %collective-permute-start.1 = (f32[2048,640]{1,0:T(8,128)}, f32[2048,640]{1,0:T(8,128)}, u32[]{:S(2)}, u32[]{:S(2)}) collective-permute-start(f32[2048,640]{1,0:T(8,128)} %get-tuple-element.206), channel_id=1, source_target_pairs={{0,1},{1,2},{2,3},{3,4},{4,5},{5,6},{6,7},{7,8},{8,9},{9,10},{10,1... | collective-permute-start | bytes 15728648 | tf_op jit(solution)/shard_map/while/body/eval_jaxpr/ppermute | solution.py:50
  377.9 32.9 %collective-permute-start = (bf16[2048,640]{1,0:T(8,128)(2,1)}, bf16[2048,640]{1,0:T(8,128)(2,1)}, u32[]{:S(2)}, u32[]{:S(2)}) collective-permute-start(bf16[2048,640]{1,0:T(8,128)(2,1)} %get-tuple-element.205), channel_id=1, source_target_pairs={{0,1},{1,2},{2,3},{3,4},{4,5},{5,6},{6,7},{7,8},{8,9},{9,10},{10,1... | collective-permute-start | bytes 7864328 | tf_op jit(solution)/shard_map/while/body/eval_jaxpr/ppermute | solution.py:49
  377.9 89.0 %collective-permute-start.1 = (f32[2048,640]{1,0:T(8,128)}, f32[2048,640]{1,0:T(8,128)}, u32[]{:S(2)}, u32[]{:S(2)}) collective-permute-start(f32[2048,640]{1,0:T(8,128)} %get-tuple-element.206), channel_id=1, source_target_pairs={{0,1},{1,2},{2,3},{3,4},{4,5},{5,6},{6,7},{7,8},{8,9},{9,10},{10,1... | collective-permute-start | bytes 15728648 | tf_op jit(solution)/shard_map/while/body/eval_jaxpr/ppermute | solution.py:50
  479.6 32.9 %collective-permute-start = (bf16[2048,640]{1,0:T(8,128)(2,1)}, bf16[2048,640]{1,0:T(8,128)(2,1)}, u32[]{:S(2)}, u32[]{:S(2)}) collective-permute-start(bf16[2048,640]{1,0:T(8,128)(2,1)} %get-tuple-element.205), channel_id=1, source_target_pairs={{0,1},{1,2},{2,3},{3,4},{4,5},{5,6},{6,7},{7,8},{8,9},{9,10},{10,1... | collective-permute-start | bytes 7864328 | tf_op jit(solution)/shard_map/while/body/eval_jaxpr/ppermute | solution.py:49
  479.6 89.0 %collective-permute-start.1 = (f32[2048,640]{1,0:T(8,128)}, f32[2048,640]{1,0:T(8,128)}, u32[]{:S(2)}, u32[]{:S(2)}) collective-permute-start(f32[2048,640]{1,0:T(8,128)} %get-tuple-element.206), channel_id=1, source_target_pairs={{0,1},{1,2},{2,3},{3,4},{4,5},{5,6},{6,7},{7,8},{8,9},{9,10},{10,1... | collective-permute-start | bytes 15728648 | tf_op jit(solution)/shard_map/while/body/eval_jaxpr/ppermute | solution.py:50
  581.4 32.9 %collective-permute-start = (bf16[2048,640]{1,0:T(8,128)(2,1)}, bf16[2048,640]{1,0:T(8,128)(2,1)}, u32[]{:S(2)}, u32[]{:S(2)}) collective-permute-start(bf16[2048,640]{1,0:T(8,128)(2,1)} %get-tuple-element.205), channel_id=1, source_target_pairs={{0,1},{1,2},{2,3},{3,4},{4,5},{5,6},{6,7},{7,8},{8,9},{9,10},{10,1... | collective-permute-start | bytes 7864328 | tf_op jit(solution)/shard_map/while/body/eval_jaxpr/ppermute | solution.py:49
  581.4 89.0 %collective-permute-start.1 = (f32[2048,640]{1,0:T(8,128)}, f32[2048,640]{1,0:T(8,128)}, u32[]{:S(2)}, u32[]{:S(2)}) collective-permute-start(f32[2048,640]{1,0:T(8,128)} %get-tuple-element.206), channel_id=1, source_target_pairs={{0,1},{1,2},{2,3},{3,4},{4,5},{5,6},{6,7},{7,8},{8,9},{9,10},{10,1... | collective-permute-start | bytes 15728648 | tf_op jit(solution)/shard_map/while/body/eval_jaxpr/ppermute | solution.py:50
  683.1 32.9 %collective-permute-start = (bf16[2048,640]{1,0:T(8,128)(2,1)}, bf16[2048,640]{1,0:T(8,128)(2,1)}, u32[]{:S(2)}, u32[]{:S(2)}) collective-permute-start(bf16[2048,640]{1,0:T(8,128)(2,1)} %get-tuple-element.205), channel_id=1, source_target_pairs={{0,1},{1,2},{2,3},{3,4},{4,5},{5,6},{6,7},{7,8},{8,9},{9,10},{10,1... | collective-permute-start | bytes 7864328 | tf_op jit(solution)/shard_map/while/body/eval_jaxpr/ppermute | solution.py:49
  683.1 89.0 %collective-permute-start.1 = (f32[2048,640]{1,0:T(8,128)}, f32[2048,640]{1,0:T(8,128)}, u32[]{:S(2)}, u32[]{:S(2)}) collective-permute-start(f32[2048,640]{1,0:T(8,128)} %get-tuple-element.206), channel_id=1, source_target_pairs={{0,1},{1,2},{2,3},{3,4},{4,5},{5,6},{6,7},{7,8},{8,9},{9,10},{10,1... | collective-permute-start | bytes 15728648 | tf_op jit(solution)/shard_map/while/body/eval_jaxpr/ppermute | solution.py:50
  784.9 89.0 %collective-permute-start.1 = (f32[2048,640]{1,0:T(8,128)}, f32[2048,640]{1,0:T(8,128)}, u32[]{:S(2)}, u32[]{:S(2)}) collective-permute-start(f32[2048,640]{1,0:T(8,128)} %get-tuple-element.206), channel_id=1, source_target_pairs={{0,1},{1,2},{2,3},{3,4},{4,5},{5,6},{6,7},{7,8},{8,9},{9,10},{10,1... | collective-permute-start | bytes 15728648 | tf_op jit(solution)/shard_map/while/body/eval_jaxpr/ppermute | solution.py:50
  886.7 89.0 %collective-permute-start.1 = (f32[2048,640]{1,0:T(8,128)}, f32[2048,640]{1,0:T(8,128)}, u32[]{:S(2)}, u32[]{:S(2)}) collective-permute-start(f32[2048,640]{1,0:T(8,128)} %get-tuple-element.206), channel_id=1, source_target_pairs={{0,1},{1,2},{2,3},{3,4},{4,5},{5,6},{6,7},{7,8},{8,9},{9,10},{10,1... | collective-permute-start | bytes 15728648 | tf_op jit(solution)/shard_map/while/body/eval_jaxpr/ppermute | solution.py:50
  988.4 89.0 %collective-permute-start.1 = (f32[2048,640]{1,0:T(8,128)}, f32[2048,640]{1,0:T(8,128)}, u32[]{:S(2)}, u32[]{:S(2)}) collective-permute-start(f32[2048,640]{1,0:T(8,128)} %get-tuple-element.206), channel_id=1, source_target_pairs={{0,1},{1,2},{2,3},{3,4},{4,5},{5,6},{6,7},{7,8},{8,9},{9,10},{10,1... | collective-permute-start | bytes 15728648 | tf_op jit(solution)/shard_map/while/body/eval_jaxpr/ppermute | solution.py:50
  1090.2 89.0 %collective-permute-start.1 = (f32[2048,640]{1,0:T(8,128)}, f32[2048,640]{1,0:T(8,128)}, u32[]{:S(2)}, u32[]{:S(2)}) collective-permute-start(f32[2048,640]{1,0:T(8,128)} %get-tuple-element.206), channel_id=1, source_target_pairs={{0,1},{1,2},{2,3},{3,4},{4,5},{5,6},{6,7},{7,8},{8,9},{9,10},{10,1... | collective-permute-start | bytes 15728648 | tf_op jit(solution)/shard_map/while/body/eval_jaxpr/ppermute | solution.py:50
  1192.0 89.0 %collective-permute-start.1 = (f32[2048,640]{1,0:T(8,128)}, f32[2048,640]{1,0:T(8,128)}, u32[]{:S(2)}, u32[]{:S(2)}) collective-permute-start(f32[2048,640]{1,0:T(8,128)} %get-tuple-element.206), channel_id=1, source_target_pairs={{0,1},{1,2},{2,3},{3,4},{4,5},{5,6},{6,7},{7,8},{8,9},{9,10},{10,1... | collective-permute-start | bytes 15728648 | tf_op jit(solution)/shard_map/while/body/eval_jaxpr/ppermute | solution.py:50
  1293.7 89.0 %collective-permute-start.1 = (f32[2048,640]{1,0:T(8,128)}, f32[2048,640]{1,0:T(8,128)}, u32[]{:S(2)}, u32[]{:S(2)}) collective-permute-start(f32[2048,640]{1,0:T(8,128)} %get-tuple-element.206), channel_id=1, source_target_pairs={{0,1},{1,2},{2,3},{3,4},{4,5},{5,6},{6,7},{7,8},{8,9},{9,10},{10,1... | collective-permute-start | bytes 15728648 | tf_op jit(solution)/shard_map/while/body/eval_jaxpr/ppermute | solution.py:50
  1395.5 89.0 %collective-permute-start.1 = (f32[2048,640]{1,0:T(8,128)}, f32[2048,640]{1,0:T(8,128)}, u32[]{:S(2)}, u32[]{:S(2)}) collective-permute-start(f32[2048,640]{1,0:T(8,128)} %get-tuple-element.206), channel_id=1, source_target_pairs={{0,1},{1,2},{2,3},{3,4},{4,5},{5,6},{6,7},{7,8},{8,9},{9,10},{10,1... | collective-permute-start | bytes 15728648 | tf_op jit(solution)/shard_map/while/body/eval_jaxpr/ppermute | solution.py:50
  1497.2 89.0 %collective-permute-start.1 = (f32[2048,640]{1,0:T(8,128)}, f32[2048,640]{1,0:T(8,128)}, u32[]{:S(2)}, u32[]{:S(2)}) collective-permute-start(f32[2048,640]{1,0:T(8,128)} %get-tuple-element.206), channel_id=1, source_target_pairs={{0,1},{1,2},{2,3},{3,4},{4,5},{5,6},{6,7},{7,8},{8,9},{9,10},{10,1... | collective-permute-start | bytes 15728648 | tf_op jit(solution)/shard_map/while/body/eval_jaxpr/ppermute | solution.py:50
  1605.2 61.0 %collective-permute-start.2 = (f32[2048,640]{0,1:T(8,128)}, f32[2048,640]{0,1:T(8,128)}, u32[]{:S(2)}, u32[]{:S(2)}) collective-permute-start(f32[2048,640]{0,1:T(8,128)} %copy.14), channel_id=1, source_target_pairs={{0,1},{1,2},{2,3},{3,4},{4,5},{5,6},{6,7},{7,8},{8,9},{9,10},{10,1... | collective-permute-start | bytes 15728648 | tf_op jit(solution)/shard_map/ppermute | solution.py:56
  (100 other events, 2399.9 us)
Sparse Core Ops, SparseCore 0:
  1689.7 76.3 all-reduce.3
where the time goes:
time: 1790 us; the launch traced here: 1780 us
  matrix products  847 us (47%)
  waiting for transfers between devices  708 us (40%)
  local copies, waits for them, and re-layouts  80.9 us (5%)
  loops' own time  77.7 us (4%)
  blocking collectives  33.2 us (2%)
  between operations  19.7 us (1%)
    ppermute x15, waiting for transfers between devices, hop(): txt_blk = lax.ppermute(txt_blk, batch_axes, next_perm)  490 us
    dot_general x16, matrix products, tile_terms(): jnp.einsum('id,jd->ij', img_emb, txt_blk, preferred_element_type=jnp.floa...  423 us
    dot_general x16, matrix products, tile_terms(): d_img = jnp.dot(grad_b, txt_blk, preferred_element_type=jnp.float32)  228 us
    dot_general x16, matrix products, tile_terms(): jnp.einsum('ij,id->jd', grad_b, img_emb, preferred_element_type=jnp.float32)  176 us
    ppermute x15, waiting for transfers between devices, hop(): d_txt_acc = lax.ppermute(d_txt_acc, batch_axes, next_perm)  120 us
    another operation x1, loops' own time, local_fn(): final_state = lax.fori_loop(1, dev_count, hop, init_state)  77.7 us
    ppermute x1, waiting for transfers between devices, local_fn(): d_txt_home = lax.ppermute(final_state[1], batch_axes, next_perm)  55 us
    while x165, local copies, waits for them, and re-layouts  54.7 us
  transfers between devices with their start and end apart: 32, of which 32 were waited for; matrix products, arithmetic and copies ran while one was open for 38% of the time, Pallas kernels for 0%

commit v1 on v0

v1 whole, which is shorter than its diff:
```python
import functools

import jax
import jax.numpy as jnp
from jax import lax
from jax.experimental import pallas as pl
from jax.experimental.pallas import tpu as pltpu
from jax.sharding import PartitionSpec as P

F32 = jnp.float32
BF16 = jnp.bfloat16
NN = (((1,), (0,)), ((), ()))
NT = (((1,), (1,)), ((), ()))
LOG2E = 1.4426950408889634
LN2 = 0.6931471805599453
BM, BN, QR = 1024, 512, 16


def dot(a, b, dims=NN):
    return lax.dot_general(a, b, dims, preferred_element_type=F32)


def tile_kernel(diag, has_di, has_dt, *refs):
    refs = list(refs)
    sc_ref, st_in, i_ref, it_ref, ta_ref, tb_ref = refs[:6]
    refs = refs[6:]
    di_in = refs.pop(0) if has_di else None
    dt_in = (refs.pop(0), refs.pop(0)) if has_dt else None
    st_ref, di_ref, dta_ref, dtb_ref, s_buf, g_buf = refs
    step = pl.program_id(0)
    scale, shift = sc_ref[0], sc_ref[1]
    half = ta_ref.shape[1]
    per = half // BN
    chunks = 2 * per

    @pl.when(step == 0)
    def _():
        st_ref[...] = st_in[...]
        for k, out in enumerate((dta_ref, dtb_ref)):
            out[...] = dt_in[k][...] if has_dt else jnp.zeros_like(out)

    def place(c):
        return c // per, pl.ds((c % per) * BN, BN)

    def similarity(c):
        k, cols = place(c)
        s_buf[c % 2] = dot(i_ref[...], (ta_ref, tb_ref)[k][:, cols])

    def pointwise(c):
        over, prod, gsum, gdot = (jnp.zeros((QR, BN), F32) for _ in range(4))
        for r in range(BM // QR):
            rows = pl.ds(r * QR, QR)
            s = s_buf[c % 2, rows, :]
            z = s * scale + shift
            e = jnp.exp2(-jnp.abs(z))
            u = 1.0 + e
            inv = 1.0 / u
            if diag:
                row_id = lax.broadcasted_iota(jnp.int32, (QR, BN), 0) + (r * QR + step * BM)
                col_id = lax.broadcasted_iota(jnp.int32, (QR, BN), 1) + c * BN
                same = row_id == col_id
                z = jnp.where(same, -z, z)
            g = jnp.where(z >= 0, inv, e * inv)
            if diag:
                g = jnp.where(same, -g, g)
            g_buf[c % 2, rows, :] = g.astype(BF16)
            over = over + jnp.maximum(z, 0.0)
            prod = e + prod * u
            gsum = gsum + g
            gdot = gdot + g * s
        st_ref[0] += over
        st_ref[1] += jnp.log1p(prod)
        st_ref[2] += gsum
        st_ref[3] += gdot

    def gradients(c):
        k, cols = place(c)
        g = g_buf[c % 2]
        t_ref, dt_ref = (ta_ref, tb_ref)[k], (dta_ref, dtb_ref)[k]
        dt_ref[:, cols] += dot(it_ref[...], g)
        part = dot(t_ref[:, cols], g, NT)
        if c:
            di_ref[...] += part
        elif has_di:
            di_ref[...] = di_in[...] + part
        else:
            di_ref[...] = part

    for c in range(chunks + 2):
        if c < chunks:
            similarity(c)
        if 1 <= c <= chunks:
            pointwise(c - 1)
        if c >= 2:
            gradients(c - 2)


def tiles(name, sc, st, img, img_t, txt, di=None, dt=None, diag=False):
    rows, dim = img.shape
    half = txt[0].shape[1]
    whole = lambda shape: pl.BlockSpec(shape, lambda g: (0,) * len(shape))
    by_col = pl.BlockSpec((dim, BM), lambda g: (0, g))
    t_spec = whole((dim, half))
    operands = [sc, st, img, img_t, *txt]
    specs = [pl.BlockSpec(memory_space=pltpu.SMEM), whole(st.shape), pl.BlockSpec((BM, dim), lambda g: (g, 0)), by_col, t_spec, t_spec]
    alias = {1: 0}
    if di is not None:
        alias[len(operands)] = 1
        operands.append(di)
        specs.append(by_col)
    if dt is not None:
        for k in range(2):
            alias[len(operands)] = 2 + k
            operands.append(dt[k])
            specs.append(t_spec)
    flops = 6 * rows * 2 * half * dim
    return pl.pallas_call(
        functools.partial(tile_kernel, diag, di is not None, dt is not None),
        name=name,
        grid=(rows // BM,),
        out_shape=(
            jax.ShapeDtypeStruct(st.shape, F32),
            jax.ShapeDtypeStruct((dim, rows), F32),
            jax.ShapeDtypeStruct((dim, half), F32),
            jax.ShapeDtypeStruct((dim, half), F32),
        ),
        in_specs=specs,
        out_specs=(whole(st.shape), by_col, t_spec, t_spec),
        scratch_shapes=[pltpu.VMEM((2, BM, BN), F32), pltpu.VMEM((2, BM, BN), BF16)],
        input_output_aliases=alias,
        cost_estimate=pl.CostEstimate(flops=flops, bytes_accessed=40 * 2**20, transcendentals=0),
        compiler_params=pltpu.CompilerParams(vmem_limit_bytes=60 * 2**20, dimension_semantics=("arbitrary",)),
    )(*operands)


def embed_t(x, w):
    raw = lax.dot_general(w, x, (((0,), (1,)), ((), ())), preferred_element_type=F32)
    inv = lax.rsqrt(jnp.sum(raw * raw, axis=0, keepdims=True))
    return raw * inv, inv


def weight_grad(x, unit, inv, grad):
    raw_grad = (inv * (grad - unit * jnp.sum(unit * grad, axis=0, keepdims=True))).astype(BF16)
    return lax.dot_general(x, raw_grad, (((0,), (1,)), ((), ())), preferred_element_type=F32)


def solution(mesh):
    rep_count, data_count = mesh.shape["replica"], mesh.shape["data"]
    dev_count = rep_count * data_count
    batch_axes = ("replica", "data")
    ring = (0, 1, 3, 2)
    forward = {ring[k]: ring[(k + 1) % 4] for k in range(4)}
    ahead = [(2 * a + k, 2 * b + k) for a, b in forward.items() for k in range(2)]
    back = [(b, a) for a, b in ahead]
    swap_core = [(k, k ^ 1) for k in range(data_count)]
    swap_z = [(0, 1), (1, 0)]

    def local_fn(img_x, txt_x, w_img, w_txt, log_temp, logit_bias):
        total_rows = img_x.shape[0] * dev_count
        go = lambda pair: (lax.ppermute(pair[0], "data", ahead), lax.ppermute(pair[1], "data", back))
        core = lambda x: lax.ppermute(x, "data", swap_core)
        over_z = lambda x: lax.ppermute(x, "replica", swap_z)

        img_unit, img_inv = embed_t(img_x, w_img)
        txt_unit, txt_inv = embed_t(txt_x, w_txt)
        temp_scale = jnp.exp(log_temp[0])
        sc = jnp.stack([temp_scale * LOG2E, logit_bias[0] * LOG2E])
        img_t = img_unit.astype(BF16)
        txt_t = txt_unit.astype(BF16)
        half = txt_t.shape[1] // 2
        b0 = (txt_t[:, :half], txt_t[:, half:])
        b1 = go(b0)
        b2 = go(b1)
        b3 = go(b2)
        peer_t = core(img_t)
        far_t = over_z(img_t)
        far_peer_t = core(far_t)
        img = img_t.T
        peer = peer_t.T
        a0_t = jnp.concatenate([img_t, peer_t], axis=1)
        a1_t = jnp.concatenate([far_t, far_peer_t], axis=1)
        a0 = a0_t.T
        a1 = a1_t.T
        n = img_t.shape[1]

        st = jnp.zeros((4, QR, BN), F32)
        st, di_own, dt0a, dt0b = tiles("own", sc, st, img, img_t, b0, diag=True)
        st, di0, *dt1 = tiles("near1", sc, st, a0, a0_t, b1)
        st, di1, *dt1 = tiles("far1", sc, st, a1, a1_t, b1, dt=dt1)
        dt1 = go(dt1)
        st, di1, *dt2 = tiles("far2", sc, st, a1, a1_t, b2, di=di1)
        st, di1, *dt0 = tiles("far0", sc, st, a1, a1_t, b0, di=di1, dt=(dt0a, dt0b))
        dt2 = (dt1[0] + dt2[0], dt1[1] + dt2[1])
        st, di0, *dt2 = tiles("near2", sc, st, a0, a0_t, b2, di=di0, dt=dt2)
        dt2 = go(dt2)
        st, di1, *dt3 = tiles("far3", sc, st, a1, a1_t, b3, di=di1)
        far_sum = di1[:, :n] + core(di1[:, n:])
        far_sum = over_z(far_sum)
        st, di0, *dt3 = tiles("near3", sc, st, a0, a0_t, b3, di=di0, dt=dt3)
        dt3 = go((dt3[0] + dt2[0], dt3[1] + dt2[1]))
        st, di_peer, *dt0 = tiles("peer0", sc, st, peer, peer_t, b0, dt=dt0)
        d_img = di_own + di0[:, :n] + core(di0[:, n:] + di_peer) + far_sum
        d_txt = jnp.concatenate([dt0[0] + dt3[0], dt0[1] + dt3[1]], axis=1)

        scale = temp_scale / total_rows
        d_w_txt = weight_grad(txt_x, txt_unit, txt_inv, scale * d_txt)
        d_w_img = weight_grad(img_x, img_unit, img_inv, scale * d_img)
        sums = jnp.sum(st, axis=(1, 2))
        loss_sum = sums[0] * LN2 + sums[1]
        totals = jnp.stack([loss_sum / total_rows, temp_scale * sums[3] / total_rows, sums[2] / total_rows])
        totals, d_w_txt = lax.psum((totals, d_w_txt), batch_axes)
        d_w_img = lax.psum(d_w_img, batch_axes)
        return totals[0:1], totals[1:2], totals[2:3], d_w_img, d_w_txt

    batch_spec = P(batch_axes, None)
    return jax.shard_map(local_fn, mesh=mesh, in_specs=(batch_spec, batch_spec, P(), P(), P(), P()), out_specs=(P(), P(), P(), P(), P()), check_vma=False)
```

time: 1790 us -> 721 us (0.40)
  matrix products: 847 us -> 13.1 us
  waiting for transfers between devices: 708 us -> 153 us
  Pallas kernels: 0 us -> 375 us
  loops' own time: 77.7 us -> 0 us
  other arithmetic: 11 us -> 52.3 us
  local copies, waits for them, and re-layouts: 80.9 us -> 51 us
    dot_general x52 -> x4, matrix products: 847 us -> 13.1 us  [the longest x2 7.38 us: weight_grad(): lax.dot_general(x, raw_grad, (((0,), (1,)), ((), ())), preferred_element_...]
    ppermute x31 -> x18, waiting for transfers between devices: 666 us -> 112 us  [the longest x6 66.5 us: local_fn(): lax.ppermute(pair[0], 'data', ahead)]
    pallas_call x0 -> x9, Pallas kernels: none -> 375 us  [tiles(): pl.pallas_call(functools.partial(tile_kernel, diag, di is not None, dt is...]
    another operation x1 -> x0, loops' own time: 77.7 us -> none  [local_fn(): final_state = lax.fori_loop(1, dev_count, hop, init_state)]
    while x169 -> x0, local copies, waits for them, and re-layouts: 75.3 us -> none
    add x0 -> x8, other arithmetic: none -> 27.6 us  [the longest x2 8.8 us: local_fn(): dt2 = (dt1[0] + dt2[0], dt1[1] + dt2[1])]
    transpose x0 -> x3, local copies, waits for them, and re-layouts: none -> 20.3 us  [the longest x1 7.88 us: local_fn(): a1 = a1_t.T]
  transfers between devices with their start and end apart: 32 -> 19, of which waited for: 32 -> 5; matrix products, arithmetic and copies ran while one was open for 38% -> 12% of each run, Pallas kernels for 0% -> 52%
where the time goes in v1:
time: 721 us; the launch traced here: 714 us
  Pallas kernels  375 us (52%)
  waiting for transfers between devices  153 us (21%)
  other arithmetic  52.3 us (7%)
  local copies, waits for them, and re-layouts  51 us (7%)
  blocking collectives  33.3 us (5%)
  between operations  18.8 us (3%)
  starting transfers between devices  18.2 us (3%)
  matrix products  13.1 us (2%)
    pallas_call x9, Pallas kernels, tiles(): pl.pallas_call(functools.partial(tile_kernel, diag, di is not None, dt is...  375 us
    ppermute x6, waiting for transfers between devices, local_fn(): lax.ppermute(pair[0], 'data', ahead)  66.5 us
    ppermute x2, waiting for transfers between devices, local_fn(): over_z = lambda x: lax.ppermute(x, 'replica', swap_z)  42.5 us
    psum x1, waiting for transfers between devices, local_fn(): d_w_img = lax.psum(d_w_img, batch_axes)  40.9 us
    psum x1, blocking collectives, local_fn(): totals, d_w_txt = lax.psum((totals, d_w_txt), batch_axes)  33.3 us
  transfers between devices with their start and end apart: 19, of which 5 were waited for; matrix products, arithmetic and copies ran while one was open for 12% of the time, Pallas kernels for 52%

profile of v1, /device:TPU:0, one launch (start us, length us, event | category | flops | bytes accessed | tf_op | source)
XLA Modules:
  0.0 714.4 jit_solution(7998372404205688868)
XLA Ops:
  30.3 5.0 copy.35.refs_2_
  35.8 12.6 %collective-permute-done.1.refs_4_ = bf16[640,1024]{1,0:T(8,128)(2,1)} collective-permute-done((bf16[640,1024]{1,0:T(8,128)(2,1)}, bf16[640,1024]{1,0:T(8,128)(2,1)}, u32[]{:S(2)}, u32[]{:S(2)}) %collective-permute-start.1) | collective-permute-done | bytes 1310752 | tf_op jit(solution)/shard_map/ppermute | solution.py:160
  51.1 26.2 %own.1 = (f32[4,16,512]{2,1,0:T(8,128)}, f32[640,2048]{1,0:T(8,128)}, f32[640,1024]{1,0:T(8,128)}, f32[640,1024]{1,0:T(8,128)}) custom-call(f32[2]{0:T(128)} %pad_maximum_fusion.1.refs_0_, f32[4,16,512]{2,1,0:T(8,128)} %broadcast_in_dim.2.refs_1_, bf16[2048,640]{1,0:T(8,128)(2,1)} %copy.35.refs_2_, ...), custom_call_target="tpu_custom_call", output_to_operand_aliasing={{0}: (1, {})} | custom-call | flops 16106127360 | bytes 41943040 | tf_op jit(solution)/shard_map/own/pallas_call | solution.py:117
  77.2 7.9 %pad_maximum_fusion = (bf16[640,4096]{1,0:T(8,128)(2,1)}, bf16[4096,640]{0,1:T(8,128)(2,1)}) fusion(bf16[640,2048]{1,0:T(8,128)(2,1)} %collective-permute-done.refs_3_, bf16[640,2048]{1,0:T(8,128)(2,1)} %multiply_convert_fusion.3.refs_3_), kind=kLoop, calls=%fused_computation | loop fusion | flops 10485760 | bytes 15728640 | tf_op jit(solution)/shard_map/concatenate | solution.py:180
  85.1 7.9 %copy.36.refs_2_ = bf16[4096,640]{1,0:T(8,128)(2,1)} copy(bf16[4096,640]{0,1:T(8,128)(2,1)} %get-tuple-element.87) | data formatting | bytes 10485760 | tf_op jit(solution)/shard_map/transpose | solution.py:182
  93.0 4.6 copy.43.refs_2_
  103.3 43.9 %near1.1 = (f32[4,16,512]{2,1,0:T(8,128)}, f32[640,4096]{1,0:T(8,128)}, f32[640,1024]{1,0:T(8,128)}, f32[640,1024]{1,0:T(8,128)}) custom-call(f32[2]{0:T(128)} %pad_maximum_fusion.1.refs_0_, f32[4,16,512]{2,1,0:T(8,128)} %get-tuple-element.41.refs_1_, bf16[4096,640]{1,0:T(8,128)(2,1)} %copy.36.refs_2_, ...), custom_call_target="tpu_custom_call", output_to_operand_aliasing={{0}: (1, {})} | custom-call | flops 32212254720 | bytes 41943040 | tf_op jit(solution)/shard_map/near1/pallas_call | solution.py:117
  150.9 7.9 %copy.37.refs_2_ = bf16[4096,640]{1,0:T(8,128)(2,1)} copy(bf16[4096,640]{0,1:T(8,128)(2,1)} %bitcast.21) | data formatting | bytes 10485760 | tf_op jit(solution)/shard_map/transpose | solution.py:183
  158.8 45.8 %far1.1 = (f32[4,16,512]{2,1,0:T(8,128)}, f32[640,4096]{1,0:T(8,128)}, f32[640,1024]{1,0:T(8,128)}, f32[640,1024]{1,0:T(8,128)}) custom-call(f32[2]{0:T(128)} %pad_maximum_fusion.1.refs_0_, f32[4,16,512]{2,1,0:T(8,128)} %get-tuple-element.42.refs_1_, bf16[4096,640]{1,0:T(8,128)(2,1)} %copy.37.refs_2_, ...), custom_call_target="tpu_custom_call", output_to_operand_aliasing={{0}: (1, {}), {2}: (6, {}), {3}: (7, {})} | custom-call | flops 32212254720 | bytes 41943040 | tf_op jit(solution)/shard_map/far1/pallas_call | solution.py:117
  206.6 45.7 %far2.1 = (f32[4,16,512]{2,1,0:T(8,128)}, f32[640,4096]{1,0:T(8,128)}, f32[640,1024]{1,0:T(8,128)}, f32[640,1024]{1,0:T(8,128)}) custom-call(f32[2]{0:T(128)} %pad_maximum_fusion.1.refs_0_, f32[4,16,512]{2,1,0:T(8,128)} %get-tuple-element.45.refs_1_, bf16[4096,640]{1,0:T(8,128)(2,1)} %copy.37.refs_2_, ...), custom_call_target="tpu_custom_call", output_to_operand_aliasing={{0}: (1, {}), {1}: (6, {})} | custom-call | flops 32212254720 | bytes 41943040 | tf_op jit(solution)/shard_map/far2/pallas_call | solution.py:117
  252.3 47.1 %far0.1 = (f32[4,16,512]{2,1,0:T(8,128)}, f32[640,4096]{1,0:T(8,128)}, f32[640,1024]{1,0:T(8,128)}, f32[640,1024]{1,0:T(8,128)}) custom-call(f32[2]{0:T(128)} %pad_maximum_fusion.1.refs_0_, f32[4,16,512]{2,1,0:T(8,128)} %get-tuple-element.47.refs_1_, ...), custom_call_target="tpu_custom_call", output_to_operand_aliasing={{0}: (1, {}), {1}: (6, {}), {2}: (7, {}), {3}: (8, {})} | custom-call | flops 32212254720 | bytes 41943040 | tf_op jit(solution)/shard_map/far0/pallas_call | solution.py:117
  299.4 4.9 add.44.refs_8_
  308.2 47.1 %near2.1 = (f32[4,16,512]{2,1,0:T(8,128)}, f32[640,4096]{1,0:T(8,128)}, f32[640,1024]{1,0:T(8,128)}, f32[640,1024]{1,0:T(8,128)}) custom-call(f32[2]{0:T(128)} %pad_maximum_fusion.1.refs_0_, f32[4,16,512]{2,1,0:T(8,128)} %get-tuple-element.51.refs_1_, ...), custom_call_target="tpu_custom_call", output_to_operand_aliasing={{0}: (1, {}), {1}: (6, {}), {2}: (7, {}), {3}: (8, {})} | custom-call | flops 32212254720 | bytes 41943040 | tf_op jit(solution)/shard_map/near2/pallas_call | solution.py:117
  357.4 45.7 %far3.1 = (f32[4,16,512]{2,1,0:T(8,128)}, f32[640,4096]{1,0:T(8,128)}, f32[640,1024]{1,0:T(8,128)}, f32[640,1024]{1,0:T(8,128)}) custom-call(f32[2]{0:T(128)} %pad_maximum_fusion.1.refs_0_, f32[4,16,512]{2,1,0:T(8,128)} %get-tuple-element.57.refs_1_, bf16[4096,640]{1,0:T(8,128)(2,1)} %copy.37.refs_2_, ...), custom_call_target="tpu_custom_call", output_to_operand_aliasing={{0}: (1, {}), {1}: (6, {})} | custom-call | flops 32212254720 | bytes 41943040 | tf_op jit(solution)/shard_map/far3/pallas_call | solution.py:117
  403.1 5.4 slice.51
  408.5 47.1 %near3.1 = (f32[4,16,512]{2,1,0:T(8,128)}, f32[640,4096]{1,0:T(8,128)}, f32[640,1024]{1,0:T(8,128)}, f32[640,1024]{1,0:T(8,128)}) custom-call(f32[2]{0:T(128)} %pad_maximum_fusion.1.refs_0_, f32[4,16,512]{2,1,0:T(8,128)} %get-tuple-element.59.refs_1_, ...), custom_call_target="tpu_custom_call", output_to_operand_aliasing={{0}: (1, {}), {1}: (6, {}), {2}: (7, {}), {3}: (8, {})} | custom-call | flops 32212254720 | bytes 41943040 | tf_op jit(solution)/shard_map/near3/pallas_call | solution.py:117
  455.6 26.4 %peer0.1 = (f32[4,16,512]{2,1,0:T(8,128)}, f32[640,2048]{1,0:T(8,128)}, f32[640,1024]{1,0:T(8,128)}, f32[640,1024]{1,0:T(8,128)}) custom-call(f32[2]{0:T(128)} %pad_maximum_fusion.1.refs_0_, f32[4,16,512]{2,1,0:T(8,128)} %get-tuple-element.63.refs_1_, bf16[2048,640]{1,0:T(8,128)(2,1)} %copy.43.refs_2_, ...), custom_call_target="tpu_custom_call", output_to_operand_aliasing={{0}: (1, {}), {2}: (6, {}), {3}: (7, {})} | custom-call | flops 16106127360 | bytes 41943040 | tf_op jit(solution)/shard_map/peer0/pallas_call | solution.py:117
  481.9 5.1 slice_add_fusion.1
  487.5 8.1 %slice_add_fusion = f32[640,2048]{1,0:T(8,128)} fusion(f32[640,2048]{1,0:T(8,128)} %collective-permute-done.12, f32[640,4096]{1,0:T(8,128)} %get-tuple-element.70), kind=kLoop, calls=%fused_computation.7 | loop fusion | flops 1310720 | bytes 15728640 | tf_op jit(solution)/shard_map/add | solution.py:197
  504.4 53.9 %collective-permute-done.15 = f32[640,1024]{1,0:T(8,128)S(1)} collective-permute-done((f32[640,1024]{1,0:T(8,128)S(1)}, f32[640,1024]{1,0:T(8,128)S(1)}, u32[]{:S(2)}, u32[]{:S(2)}) %collective-permute-start.15) | collective-permute-done | bytes 2621472 | tf_op jit(solution)/shard_map/ppermute | solution.py:160
  568.1 42.5 %collective-permute-done.13 = f32[640,2048]{1,0:T(8,128)} collective-permute-done((f32[640,2048]{1,0:T(8,128)}, f32[640,2048]{1,0:T(8,128)}, u32[]{:S(2)}, u32[]{:S(2)}) %collective-permute-start.13) | collective-permute-done | bytes 5242912 | tf_op jit(solution)/shard_map/ppermute | solution.py:162
  610.6 9.1 %multiply_reduce_fusion.1 = (f32[2048]{0:T(1024)S(1)}, f32[640,2048]{1,0:T(8,128)S(1)}) fusion(f32[640,2048]{1,0:T(8,128)S(1)} %bitcast.18, f32[2048]{0:T(1024)S(1)} %copy-done.10, f32[640,2048]{1,0:T(8,128)} %collective-permute-done.13, f32[640,2048]{1,0:T(8,128)} %collective-permute-done.11, f32[640,2048]{1,0:T(8,128)} %get-tuple-element.67, ...), kind=kLoop, calls=%fused_computation.5 | loop fusion | flops 9172992 | bytes 31473668 | tf_op jit(solution)/shard_map/reduce_sum | solution.py:143
  626.7 33.3 %psum.21 = f32[3]{0:T(128)S(1)} all-reduce(f32[3]{0:T(128)S(1)} %pad_maximum_fusion.2), channel_id=1, replica_groups=mesh['replica'=2,'data'=8] {'replica','data'}, use_global_device_ids=true, to_apply=%region_3.0 | all-reduce | flops 3 | bytes 24 | tf_op jit(solution)/shard_map/psum | solution.py:211
  660.7 40.9 %all-reduce.3.cloned.1.call-done = (f32[640,640]{0,1:T(8,128)}, f32[768,640]{0,1:T(8,128)}) async-done(((f32[640,640]{0,1:T(8,128)}, f32[768,640]{0,1:T(8,128)}), (f32[640,640]{0,1:T(8,128)}, f32[768,640]{0,1:T(8,128)})) %all-reduce.3.cloned.1.call-update) | async-done | bytes 3604496 | tf_op jit(solution)/shard_map/psum | solution.py:212
  (103 shorter events, 71.8 us)
Async XLA Ops:
  7.2 694.4 %all-reduce.3.cloned.1.call-start = ((), (), s32[]{:S(2)}) async-start(), calls=%async_computation | async-start | bytes 7208960 | tf_op jit(solution)/shard_map/psum | solution.py:212
  16.3 32.0 %collective-permute-start.1 = (bf16[640,1024]{1,0:T(8,128)(2,1)}, bf16[640,1024]{1,0:T(8,128)(2,1)}, u32[]{:S(2)}, u32[]{:S(2)}) collective-permute-start(bf16[640,1024]{1,0:T(8,128)(2,1)} %get-tuple-element.89.refs_4_), channel_id=1, source_target_pairs={{0,2},{1,3},{2,6},{3,7},{6,4},{7,5},{4,0},{5,1},{8,10},{9,11},{10,... | collective-permute-start | bytes 3932168 | tf_op jit(solution)/shard_map/ppermute | solution.py:160
  19.6 30.5 %collective-permute-start.2 = (bf16[640,1024]{1,0:T(8,128)(2,1)}, bf16[640,1024]{1,0:T(8,128)(2,1)}, u32[]{:S(2)}, u32[]{:S(2)}) collective-permute-start(bf16[640,1024]{1,0:T(8,128)(2,1)} %get-tuple-element.88.refs_5_), channel_id=1, source_target_pairs={{2,0},{3,1},{6,2},{7,3},{4,6},{5,7},{0,4},{1,5},{10,8},{11,9},{14,... | collective-permute-start | bytes 3932168 | tf_op jit(solution)/shard_map/ppermute | solution.py:160
  24.6 52.6 %collective-permute-start = (bf16[640,2048]{1,0:T(8,128)(2,1)}, bf16[640,2048]{1,0:T(8,128)(2,1)}, u32[]{:S(2)}, u32[]{:S(2)}) collective-permute-start(bf16[640,2048]{1,0:T(8,128)(2,1)} %multiply_convert_fusion.3.refs_3_), channel_id=1, source_target_pairs={{0,1},{1,0},{2,3},{3,2},{4,5},{5,4},{6,7},{7,6},{8,9},{9,8},{10,11... | collective-permute-start | bytes 7864328 | tf_op jit(solution)/shard_map/ppermute | solution.py:161
  24.6 72.9 %collective-permute-start.3 = (bf16[640,2048]{1,0:T(8,128)(2,1)}, bf16[640,2048]{1,0:T(8,128)(2,1)}, u32[]{:S(2)}, u32[]{:S(2)}) collective-permute-start(bf16[640,2048]{1,0:T(8,128)(2,1)} %multiply_convert_fusion.3.refs_3_), channel_id=1, source_target_pairs={{0,8},{8,0},{1,9},{9,1},{2,10},{10,2},{3,11},{11,3},{4,12},{12,4},... | collective-permute-start | bytes 7864328 | tf_op jit(solution)/shard_map/ppermute | solution.py:162
  48.4 54.7 %collective-permute-start.5 = (bf16[640,1024]{1,0:T(8,128)(2,1)}, bf16[640,1024]{1,0:T(8,128)(2,1)}, u32[]{:S(2)}, u32[]{:S(2)}) collective-permute-start(bf16[640,1024]{1,0:T(8,128)(2,1)} %collective-permute-done.1.refs_4_), channel_id=1, source_target_pairs={{0,2},{1,3},{2,6},{3,7},{6,4},{7,5},{4,0},{5,1},{8,10},{9,11},{10,... | collective-permute-start | bytes 3932168 | tf_op jit(solution)/shard_map/ppermute | solution.py:160
  50.1 47.5 %collective-permute-start.6 = (bf16[640,1024]{1,0:T(8,128)(2,1)}, bf16[640,1024]{1,0:T(8,128)(2,1)}, u32[]{:S(2)}, u32[]{:S(2)}) collective-permute-start(bf16[640,1024]{1,0:T(8,128)(2,1)} %collective-permute-done.2.refs_5_), channel_id=1, source_target_pairs={{2,0},{3,1},{6,2},{7,3},{4,6},{5,7},{0,4},{1,5},{10,8},{11,9},{14,... | collective-permute-start | bytes 3932168 | tf_op jit(solution)/shard_map/ppermute | solution.py:160
  97.6 49.7 %collective-permute-start.4 = (bf16[640,2048]{1,0:T(8,128)(2,1)}, bf16[640,2048]{1,0:T(8,128)(2,1)}, u32[]{:S(2)}, u32[]{:S(2)}) collective-permute-start(bf16[640,2048]{1,0:T(8,128)(2,1)} %collective-permute-done.3), channel_id=1, source_target_pairs={{0,1},{1,0},{2,3},{3,2},{4,5},{5,4},{6,7},{7,6},{8,9},{9,8},{10,11... | collective-permute-start | bytes 7864328 | tf_op jit(solution)/shard_map/ppermute | solution.py:161
  97.6 259.7 %collective-permute-start.10 = (bf16[640,1024]{1,0:T(8,128)(2,1)}, bf16[640,1024]{1,0:T(8,128)(2,1)}, u32[]{:S(2)}, u32[]{:S(2)}) collective-permute-start(bf16[640,1024]{1,0:T(8,128)(2,1)} %collective-permute-done.6.refs_5_), channel_id=1, source_target_pairs={{2,0},{3,1},{6,2},{7,3},{4,6},{5,7},{0,4},{1,5},{10,8},{11,9},{14,... | collective-permute-start | bytes 3932168 | tf_op jit(solution)/shard_map/ppermute | solution.py:160
  103.1 254.3 %collective-permute-start.9 = (bf16[640,1024]{1,0:T(8,128)(2,1)}, bf16[640,1024]{1,0:T(8,128)(2,1)}, u32[]{:S(2)}, u32[]{:S(2)}) collective-permute-start(bf16[640,1024]{1,0:T(8,128)(2,1)} %collective-permute-done.5.refs_4_), channel_id=1, source_target_pairs={{0,2},{1,3},{2,6},{3,7},{6,4},{7,5},{4,0},{5,1},{8,10},{9,11},{10,... | collective-permute-start | bytes 3932168 | tf_op jit(solution)/shard_map/ppermute | solution.py:160
  204.6 94.8 %collective-permute-start.8 = (f32[640,1024]{1,0:T(8,128)}, f32[640,1024]{1,0:T(8,128)}, u32[]{:S(2)}, u32[]{:S(2)}) collective-permute-start(f32[640,1024]{1,0:T(8,128)} %get-tuple-element.55), channel_id=1, source_target_pairs={{2,0},{3,1},{6,2},{7,3},{4,6},{5,7},{0,4},{1,5},{10,8},{11,9},{14,... | collective-permute-start | bytes 7864328 | tf_op jit(solution)/shard_map/ppermute | solution.py:160
  206.3 98.0 %collective-permute-start.7 = (f32[640,1024]{1,0:T(8,128)}, f32[640,1024]{1,0:T(8,128)}, u32[]{:S(2)}, u32[]{:S(2)}) collective-permute-start(f32[640,1024]{1,0:T(8,128)} %get-tuple-element.53), channel_id=1, source_target_pairs={{0,2},{1,3},{2,6},{3,7},{6,4},{7,5},{4,0},{5,1},{8,10},{9,11},{10,... | collective-permute-start | bytes 7864328 | tf_op jit(solution)/shard_map/ppermute | solution.py:160
  355.3 142.1 %collective-permute-start.14 = (f32[640,1024]{1,0:T(8,128)}, f32[640,1024]{1,0:T(8,128)}, u32[]{:S(2)}, u32[]{:S(2)}) collective-permute-start(f32[640,1024]{1,0:T(8,128)} %get-tuple-element.73), channel_id=1, source_target_pairs={{0,2},{1,3},{2,6},{3,7},{6,4},{7,5},{4,0},{5,1},{8,10},{9,11},{10,... | collective-permute-start | bytes 7864328 | tf_op jit(solution)/shard_map/ppermute | solution.py:160
  357.1 144.2 %collective-permute-start.16 = (f32[640,1024]{1,0:T(8,128)}, f32[640,1024]{1,0:T(8,128)}, u32[]{:S(2)}, u32[]{:S(2)}) collective-permute-start(f32[640,1024]{1,0:T(8,128)} %get-tuple-element.76), channel_id=1, source_target_pairs={{2,0},{3,1},{6,2},{7,3},{4,6},{5,7},{0,4},{1,5},{10,8},{11,9},{14,... | collective-permute-start | bytes 7864328 | tf_op jit(solution)/shard_map/ppermute | solution.py:160
  408.5 79.0 %collective-permute-start.12 = (f32[640,2048]{1,0:T(8,128)}, f32[640,2048]{1,0:T(8,128)}, u32[]{:S(2)}, u32[]{:S(2)}) collective-permute-start(f32[640,2048]{1,0:T(8,128)} %slice.51), channel_id=1, source_target_pairs={{0,1},{1,0},{2,3},{3,2},{4,5},{5,4},{6,7},{7,6},{8,9},{9,8},{10,11... | collective-permute-start | bytes 15728648 | tf_op jit(solution)/shard_map/ppermute | solution.py:161
  487.0 81.1 %collective-permute-start.11 = (f32[640,2048]{1,0:T(8,128)S(1)}, f32[640,2048]{1,0:T(8,128)}, u32[]{:S(2)}, u32[]{:S(2)}) collective-permute-start(f32[640,2048]{1,0:T(8,128)S(1)} %slice_add_fusion.1), channel_id=1, source_target_pairs={{0,1},{1,0},{2,3},{3,2},{4,5},{5,4},{6,7},{7,6},{8,9},{9,8},{10,11... | collective-permute-start | bytes 15728648 | tf_op jit(solution)/shard_map/ppermute | solution.py:161
  495.7 115.0 %collective-permute-start.13 = (f32[640,2048]{1,0:T(8,128)}, f32[640,2048]{1,0:T(8,128)}, u32[]{:S(2)}, u32[]{:S(2)}) collective-permute-start(f32[640,2048]{1,0:T(8,128)} %slice_add_fusion), channel_id=1, source_target_pairs={{0,8},{8,0},{1,9},{9,1},{2,10},{10,2},{3,11},{11,3},{4,12},{12,4},... | collective-permute-start | bytes 15728648 | tf_op jit(solution)/shard_map/ppermute | solution.py:162
  499.7 58.5 %copy-start.3 = (f32[640,1024]{1,0:T(8,128)S(1)}, f32[640,1024]{1,0:T(8,128)}, u32[]{:S(2)}) copy-start(f32[640,1024]{1,0:T(8,128)} %get-tuple-element.71) | copy-start | bytes 7864324
  499.8 58.5 %collective-permute-start.15 = (f32[640,1024]{1,0:T(8,128)S(1)}, f32[640,1024]{1,0:T(8,128)S(1)}, u32[]{:S(2)}, u32[]{:S(2)}) collective-permute-start(f32[640,1024]{1,0:T(8,128)S(1)} %add.51), channel_id=1, source_target_pairs={{0,2},{1,3},{2,6},{3,7},{6,4},{7,5},{4,0},{5,1},{8,10},{9,11},{10,... | collective-permute-start | bytes 7864328 | tf_op jit(solution)/shard_map/ppermute | solution.py:160
  503.6 58.2 %copy-start.4 = (f32[640,1024]{1,0:T(8,128)S(1)}, f32[640,1024]{1,0:T(8,128)}, u32[]{:S(2)}) copy-start(f32[640,1024]{1,0:T(8,128)} %get-tuple-element.74) | copy-start | bytes 7864324
  503.6 58.2 %collective-permute-start.17 = (f32[640,1024]{1,0:T(8,128)S(1)}, f32[640,1024]{1,0:T(8,128)S(1)}, u32[]{:S(2)}, u32[]{:S(2)}) collective-permute-start(f32[640,1024]{1,0:T(8,128)S(1)} %add.53), channel_id=1, source_target_pairs={{2,0},{3,1},{6,2},{7,3},{4,6},{5,7},{0,4},{1,5},{10,8},{11,9},{14,... | collective-permute-start | bytes 7864328 | tf_op jit(solution)/shard_map/ppermute | solution.py:160
  563.0 47.6 %slice-start = ((s8[5242880]{0:T(1024)(128)(4,1)}), s8[4194304]{0:T(1024)(128)(4,1)S(1)}, s32[]{:S(2)}) async-start(s8[5242880]{0:T(1024)(128)(4,1)} %bitcast.17), calls=%async_computation.1 | async-start | bytes 8388608
  564.3 46.4 %slice-start.1 = ((s8[5242880]{0:T(1024)(128)(4,1)}), s8[1048576]{0:T(1024)(128)(4,1)S(1)}, s32[]{:S(2)}) async-start(s8[5242880]{0:T(1024)(128)(4,1)} %bitcast.17), calls=%async_computation.2 | async-start | bytes 2097152
  564.3 46.4 %copy-start.10 = (f32[2048]{0:T(1024)S(1)}, f32[2048]{0:T(1024)}, u32[]{:S(2)}) copy-start(f32[2048]{0:T(1024)} %copy-done.9) | copy-start | bytes 24580
  (15 other events, 80.3 us)
Sparse Core Ops, SparseCore 0:
  623.5 77.9 all-reduce.2

commit v2 on v0

v2 whole, which is shorter than its diff:
```python
import functools

import jax
import jax.numpy as jnp
from jax import lax
from jax.experimental import pallas as pl
from jax.experimental.pallas import tpu as pltpu
from jax.sharding import PartitionSpec as P

F32 = jnp.float32
BF16 = jnp.bfloat16
MESH = pl.DeviceIdType.MESH
NN = (((1,), (0,)), ((), ()))
NT = (((1,), (1,)), ((), ()))
LOG2E = 1.4426950408889634
LN2 = 0.6931471805599453
BM, HALF, BN, SN, QR = 1024, 1024, 512, 256, 16
CHUNKS, PER = 2 * HALF // BN, BN // SN
IMG_SEQ = (0, 1, 0, 2, 3, 2, 3, 0, 1, 3, 2, 3, 2, 1, 0, 1)
TXT_SEQ = (0, 1, 1, 1, 1, 2, 2, 2, 2, 3, 3, 0, 0, 3, 3, 0)
STEPS = 2 * len(IMG_SEQ)


def dot(a, b, dims=NN):
    return lax.dot_general(a, b, dims, preferred_element_type=F32)


def entry(seq, u):
    low, high = (sum(v << (2 * k) for k, v in enumerate(part)) for part in (seq[:8], seq[8:]))
    code = low + (u // 8) * (high - low)
    return (code >> (2 * (u % 8))) % 4


def is_first(n):
    return (n < 4) | ((n >= 6) & (n < 10))


def kernel(
    sc_ref, img_ref, txt_ref,
    st_ref, di_ref, dt0_ref, inc_t, inc_core, inc_z, inc_own,
    i_all, it_all, t_all, acc, slots, s_buf, g_buf,
    init_sem, load_sem, store_sem, temp_sem, far_sem, out_sem,
    t_send, t_recv, i_send, i_recv, dt_send, dt_recv, di_send, di_recv,
):
    rep, dat = lax.axis_index("replica"), lax.axis_index("data")
    y, x, core = dat // 4, (dat // 2) % 2, dat % 2
    ahead = (rep, 4 * x + 2 * (1 - y) + core)
    behind = (rep, 4 * (1 - x) + 2 * y + core)
    twin = (rep, 4 * y + 2 * x + (1 - core))
    far = (1 - rep, dat)
    scale, shift = sc_ref[0], sc_ref[1]

    def remote(src, dst, sems, k, to):
        return pltpu.make_async_remote_copy(src_ref=src, dst_ref=dst, send_sem=sems[0].at[k], recv_sem=sems[1].at[k], device_id=to, device_id_type=MESH)

    def txt_hop(s, h):
        src = txt_ref.at[h] if s == 1 else t_all.at[s - 1, h]
        return remote(src, t_all.at[s, h], (t_send, t_recv), 2 * (s - 1) + h, (ahead, behind)[h])

    def img_hop(kind, c):
        src = it_all.at[4 + c] if kind == 2 else img_ref.at[c]
        return remote(src, it_all.at[2 + 2 * kind + c], (i_send, i_recv), 2 * kind + c, (twin, far, twin)[kind])

    def dt_hop(s, h):
        return remote(acc.at[(1, 2, 1)[s], h], inc_t.at[s, h], (dt_send, dt_recv), 2 * s + h, (ahead, behind)[h])

    def di_hop(kind, c):
        src = di_ref.at[(6, 4, 2)[kind] + c]
        return remote(src, (inc_core, inc_z, inc_own)[kind].at[c], (di_send, di_recv), 2 * kind + c, (twin, far, twin)[kind])

    def add_from(dst, src):
        rows = src.shape[0]
        for first in range(0, HALF, 2 * SN):
            copies = [pltpu.make_async_copy(src.at[:, pl.ds(first + p * SN, SN)], s_buf.at[p, pl.ds(0, rows)], temp_sem.at[p]) for p in range(2)]
            for cp in copies:
                cp.start()
            for p, cp in enumerate(copies):
                cp.wait()
                cols = pl.ds(first + p * SN, SN)
                dst[:, cols] += s_buf[p, 0:rows, :]

    def load(chunk, slot):
        return pltpu.make_async_copy(di_ref.at[chunk], slots.at[slot], load_sem.at[slot])

    def store(chunk, slot):
        return pltpu.make_async_copy(slots.at[slot], di_ref.at[chunk], store_sem.at[slot])

    def chunk_of(n):
        return 2 * entry(IMG_SEQ, n // 2) + n % 2

    barrier = pltpu.get_barrier_semaphore()
    for to in (ahead, behind, twin, far):
        pl.semaphore_signal(barrier, inc=1, device_id=to, device_id_type=MESH)
    pl.semaphore_wait(barrier, 4)

    own = [pltpu.make_async_copy(img_ref.at[c], it_all.at[c], init_sem.at[c]) for c in range(2)]
    own += [pltpu.make_async_copy(txt_ref.at[h], t_all.at[0, h], init_sem.at[2 + h]) for h in range(2)]
    for cp in own:
        cp.start()
    for h in range(2):
        txt_hop(1, h).start()
    for c in range(2):
        img_hop(1, c).start()
    for c in range(2):
        img_hop(0, c).start()
    st_ref[...] = jnp.zeros_like(st_ref)
    for cp in own:
        cp.wait()

    def step(n, diag):
        tb = entry(TXT_SEQ, n // 2)
        ab = tb - 2 * (tb // 3)
        chunk, slot, after = chunk_of(n), n % 3, (n + 1) % 3

        if not diag:
            @pl.when(n == 2)
            def _():
                img_hop(0, 0).wait_recv()
                for h in range(2):
                    txt_hop(1, h).wait_recv()
                    txt_hop(2, h).start()

            @pl.when(n == 3)
            def _():
                img_hop(0, 1).wait_recv()

            @pl.when(n == 5)
            def _():
                img_hop(1, 0).wait_recv()
                img_hop(2, 0).start()

            @pl.when(n == 6)
            def _():
                for h in range(2):
                    txt_hop(2, h).wait_recv()
                    txt_hop(3, h).start()

            @pl.when(n == 7)
            def _():
                img_hop(1, 1).wait_recv()
                img_hop(2, 1).start()

            @pl.when(n == 8)
            def _():
                img_hop(2, 0).wait_recv()

            @pl.when(n == 9)
            def _():
                img_hop(2, 1).wait_recv()

            @pl.when(n == 10)
            def _():
                for h in range(2):
                    dt_hop(0, h).start()

            @pl.when(n == 18)
            def _():
                for h in range(2):
                    dt_hop(1, h).start()
                for h in range(2):
                    dt_hop(0, h).wait_send()
                    txt_hop(3, h).wait_recv()

            @pl.when(n == 30)
            def _():
                for h in range(2):
                    dt_hop(2, h).start()

        @pl.when((n == 0) | (n == 2) | (n == 10) | (n == 18))
        def _():
            acc[ab] = jnp.zeros(acc.shape[1:], F32)

        @pl.when(is_first(n))
        def _():
            i_all[chunk] = it_all[chunk].T
            slots[slot] = jnp.zeros(slots.shape[1:], F32)

        @pl.when(jnp.logical_not(is_first(n)))
        def _():
            load(chunk, slot).wait()

        @pl.when((n >= 2) & (n != 26) & (n != 27))
        def _():
            store(chunk_of(n - 2), after).wait()

        @pl.when((n < STEPS - 1) & jnp.logical_not(is_first(n + 1)))
        def _():
            load(chunk_of(n + 1), after).start()

        if not diag:
            for c in range(2):
                @pl.when(n == 24 + c)
                def _():
                    di_hop(0, c).start()

        def similarity(k):
            h, cols = (k * SN) // HALF, pl.ds((k * SN) % HALF, SN)
            s_buf[k % 2] = dot(i_all[chunk], t_all[tb, h, :, cols])

        def pointwise(k):
            over, prod, gsum, gdot = (jnp.zeros((QR, SN), F32) for _ in range(4))
            for r in range(BM // QR):
                rows = pl.ds(r * QR, QR)
                s = s_buf[k % 2, rows, :]
                z = s * scale + shift
                e = jnp.exp2(-jnp.abs(z))
                u = 1.0 + e
                inv = 1.0 / u
                if diag:
                    row_id = lax.broadcasted_iota(jnp.int32, (QR, SN), 0) + (r * QR + n * BM)
                    col_id = lax.broadcasted_iota(jnp.int32, (QR, SN), 1) + k * SN
                    same = row_id == col_id
                    z = jnp.where(same, -z, z)
                g = jnp.where(z >= 0, inv, e * inv)
                if diag:
                    g = jnp.where(same, -g, g)
                g_buf[(k // PER) % 2, rows, pl.ds((k % PER) * SN, SN)] = g.astype(BF16)
                over = over + jnp.maximum(z, 0.0)
                prod = e + prod * u
                gsum = gsum + g
                gdot = gdot + g * s
            st_ref[0] += over
            st_ref[1] += jnp.log1p(prod)
            st_ref[2] += gsum
            st_ref[3] += gdot

        def gradients(c):
            h, cols = (c * BN) // HALF, pl.ds((c * BN) % HALF, BN)
            g = g_buf[c % 2]
            acc[ab, h, :, cols] += dot(it_all[chunk], g)
            slots[slot] += dot(t_all[tb, h, :, cols], g, NT)

        for k in range(CHUNKS * PER + 1 + PER):
            if k < CHUNKS * PER:
                similarity(k)
            if 1 <= k <= CHUNKS * PER:
                pointwise(k - 1)
            if k > PER and (k - 1) % PER == 0:
                gradients((k - 1) // PER - 1)

        if not diag:
            @pl.when(n == 17)
            def _():
                for h in range(2):
                    dt_hop(0, h).wait_recv()
                    add_from(acc.at[2, h], inc_t.at[0, h])

            @pl.when(n == 29)
            def _():
                for h in range(2):
                    dt_hop(1, h).wait_recv()
                    add_from(acc.at[1, h], inc_t.at[1, h])

            for c in range(2):
                @pl.when(n == 24 + c)
                def _():
                    di_hop(0, c).wait_recv()
                    add_from(slots.at[c], inc_core.at[c])
                    to_hbm = pltpu.make_async_copy(slots.at[c], di_ref.at[4 + c], far_sem.at[c])
                    to_hbm.start()
                    to_hbm.wait()
                    di_hop(1, c).start()

        @pl.when((n != 24) & (n != 25))
        def _():
            store(chunk, slot).start()

    lax.fori_loop(0, 2, lambda n, _: step(n, True), None)
    lax.fori_loop(2, STEPS, lambda n, _: step(n, False), None)

    final = [pltpu.make_async_copy(acc.at[0, h], dt0_ref.at[h], out_sem.at[h]) for h in range(2)]
    for c in range(2):
        store(2 + c, (STEPS - 2 + c) % 3).wait()
        di_hop(2, c).start()
    for cp in final:
        cp.start()
    for s in range(1, 4):
        for h in range(2):
            txt_hop(s, h).wait_send()
    for kind in range(3):
        for c in range(2):
            img_hop(kind, c).wait_send()
    for h in range(2):
        dt_hop(1, h).wait_send()
        dt_hop(2, h).wait_send()
    for kind in range(3):
        for c in range(2):
            di_hop(kind, c).wait_send()
    for cp in final:
        cp.wait()
    for h in range(2):
        dt_hop(2, h).wait_recv()
    for kind in (1, 2):
        for c in range(2):
            di_hop(kind, c).wait_recv()


def score(sc, img_t, txt_t):
    dim = img_t.shape[1]
    any_spec = pl.BlockSpec(memory_space=pl.ANY)
    piece = (dim, HALF)
    hbm = lambda *lead: jax.ShapeDtypeStruct((*lead, *piece), F32)
    dma = lambda k: pltpu.SemaphoreType.DMA((k,))
    flops = 6 * STEPS * BM * 2 * HALF * dim
    return pl.pallas_call(
        kernel,
        name="score",
        out_shape=(jax.ShapeDtypeStruct((4, QR, SN), F32), hbm(8), hbm(2), hbm(3, 2), hbm(2), hbm(2), hbm(2)),
        in_specs=[pl.BlockSpec(memory_space=pltpu.SMEM), any_spec, any_spec],
        out_specs=(pl.BlockSpec(memory_space=pltpu.VMEM),) + (any_spec,) * 6,
        scratch_shapes=[
            pltpu.VMEM((8, BM, dim), BF16),
            pltpu.VMEM((8, dim, BM), BF16),
            pltpu.VMEM((4, 2, dim, HALF), BF16),
            pltpu.VMEM((3, 2, dim, HALF), F32),
            pltpu.VMEM((3, dim, BM), F32),
            pltpu.VMEM((2, BM, SN), F32),
            pltpu.VMEM((2, BM, BN), BF16),
            dma(4), dma(3), dma(3), dma(2), dma(2), dma(2),
            dma(6), dma(6), dma(6), dma(6), dma(6), dma(6), dma(6), dma(6),
        ],
        cost_estimate=pl.CostEstimate(flops=flops, bytes_accessed=2**28, transcendentals=0),
        compiler_params=pltpu.CompilerParams(vmem_limit_bytes=67043328, collective_id=0, has_side_effects=True),
    )(sc, img_t, txt_t)


def embed_t(x, w):
    halves = [lax.dot_general(w, x[k * HALF:(k + 1) * HALF], (((0,), (1,)), ((), ())), preferred_element_type=F32) for k in range(2)]
    raw = jnp.stack(halves)
    inv = lax.rsqrt(jnp.sum(raw * raw, axis=1, keepdims=True))
    return raw * inv, inv


def weight_grad(x, unit, inv, grad):
    raw_grad = (inv * (grad - unit * jnp.sum(unit * grad, axis=1, keepdims=True))).astype(BF16)
    parts = [lax.dot_general(x[k * HALF:(k + 1) * HALF], raw_grad[k], (((0,), (1,)), ((), ())), preferred_element_type=F32) for k in range(2)]
    return parts[0] + parts[1]


def solution(mesh):
    dev_count = mesh.shape["replica"] * mesh.shape["data"]
    batch_axes = ("replica", "data")

    def local_fn(img_x, txt_x, w_img, w_txt, log_temp, logit_bias):
        total_rows = img_x.shape[0] * dev_count
        img_unit, img_inv = embed_t(img_x, w_img)
        txt_unit, txt_inv = embed_t(txt_x, w_txt)
        temp_scale = jnp.exp(log_temp[0])
        sc = jnp.stack([temp_scale * LOG2E, logit_bias[0] * LOG2E])
        st, di, dt0, inc_t, _, inc_z, inc_own = score(sc, img_unit.astype(BF16), txt_unit.astype(BF16))
        scale = temp_scale / total_rows
        d_w_txt = weight_grad(txt_x, txt_unit, txt_inv, scale * (dt0 + inc_t[2]))
        d_w_img = weight_grad(img_x, img_unit, img_inv, scale * (di[0:2] + inc_own + inc_z))
        sums = jnp.sum(st, axis=(1, 2))
        loss_sum = sums[0] * LN2 + sums[1]
        totals = jnp.stack([loss_sum / total_rows, temp_scale * sums[3] / total_rows, sums[2] / total_rows])
        totals, d_w_txt, d_w_img = lax.psum((totals, d_w_txt, d_w_img), batch_axes)
        return totals[0:1], totals[1:2], totals[2:3], d_w_img, d_w_txt

    batch_spec = P(batch_axes, None)
    return jax.shard_map(local_fn, mesh=mesh, in_specs=(batch_spec, batch_spec, P(), P(), P(), P()), out_specs=(P(), P(), P(), P(), P()), check_vma=False)
```

time: 1790 us -> 585 us (0.33)
  matrix products: 847 us -> 15.3 us
  waiting for transfers between devices: 708 us -> 40.2 us
  Pallas kernels: 0 us -> 434 us
  loops' own time: 77.7 us -> 0 us
  local copies, waits for them, and re-layouts: 80.9 us -> 9.28 us
  other arithmetic: 11 us -> 30.4 us
    dot_general x52 -> x8, matrix products: 847 us -> 15.3 us  [the longest x4 8.69 us: weight_grad(): lax.dot_general(x[k * HALF:(k + 1) * HALF], raw_grad[k], (((0,), (1,)), (...]
    ppermute x31 -> x0, waiting for transfers between devices: 666 us -> none  [the longest x15 490 us: hop(): txt_blk = lax.ppermute(txt_blk, batch_axes, next_perm)]
    pallas_call x0 -> x1, Pallas kernels: none -> 434 us  [score(): pl.pallas_call(kernel, name='score', out_shape=(jax.ShapeDtypeStruct((4,...]
    another operation x1 -> x0, loops' own time: 77.7 us -> none  [local_fn(): final_state = lax.fori_loop(1, dev_count, hop, init_state)]
    while x169 -> x0, local copies, waits for them, and re-layouts: 75.3 us -> none
    mul x2, other arithmetic: 0.02 us -> 25.3 us  [weight_grad(): unit * jnp.sum(unit * grad, axis=1, keepdims=True)]
  transfers between devices with their start and end apart: 32 -> 1, of which waited for: 32 -> 1; matrix products, arithmetic and copies ran while one was open for 38% -> 0% of each run, Pallas kernels for 0% -> 0%
where the time goes in v2:
time: 585 us; the launch traced here: 579 us
  Pallas kernels  434 us (74%)
  waiting for transfers between devices  40.2 us (7%)
  blocking collectives  32.1 us (5%)
  other arithmetic  30.4 us (5%)
  between operations  18.7 us (3%)
  matrix products  15.3 us (3%)
  local copies, waits for them, and re-layouts  9.28 us (2%)
    pallas_call x1, Pallas kernels, score(): pl.pallas_call(kernel, name='score', out_shape=(jax.ShapeDtypeStruct((4,...  434 us
    psum x1, waiting for transfers between devices, local_fn(): totals, d_w_txt, d_w_img = lax.psum((totals, d_w_txt, d_w_img), batch_axes)  40.2 us
    psum x1, blocking collectives, local_fn(): totals, d_w_txt, d_w_img = lax.psum((totals, d_w_txt, d_w_img), batch_axes)  32.1 us
    mul x2, other arithmetic, weight_grad(): unit * jnp.sum(unit * grad, axis=1, keepdims=True)  25.3 us
  transfers between devices with their start and end apart: 1, of which 1 were waited for; matrix products, arithmetic and copies ran while one was open for 0% of the time, Pallas kernels for 0%

profile of v2, /device:TPU:0, one launch (start us, length us, event | category | flops | bytes accessed | tf_op | source)
XLA Modules:
  0.0 579.5 jit_solution(12238974288940572608)
XLA Ops:
  7.2 2.9 convolution_bitcast_fusion
  10.2 1.2 convolution_bitcast_fusion.1
  11.5 1.6 copy-done.11
  13.3 1.2 convolution_bitcast_fusion.2
  14.6 1.2 convolution_bitcast_fusion.3
  15.8 0.6 multiply_reduce_fusion.3
  16.4 0.6 multiply_reduce_fusion.2
  18.4 3.3 fusion.12
  21.6 0.6 pad_maximum_fusion.2.sc_ref
  22.2 433.5 %score.1 = (f32[4,16,256]{2,1,0:T(8,128)}, f32[8,640,1024]{2,1,0:T(8,128)}, f32[2,640,1024]{2,1,0:T(8,128)}, f32[3,2,640,1024]{3,2,1,0:T(8,128)}, f32[2,640,1024...) custom-call(f32[2]{0:T(128)} %pad_maximum_fusion.2.sc_ref, ...), custom_call_target="tpu_custom_call" | custom-call | flops 257698037760 | bytes 268435456 | tf_op jit(solution)/shard_map/score/pallas_call | solution.py:305
  455.7 12.3 %multiply_convert_fusion = bf16[2,640,1024]{2,1,0:T(8,128)(2,1)S(1)} fusion(f32[1,640,1024]{2,1,0:T(8,128)} %copy-done.4, f32[1,640,1024]{2,1,0:T(8,128)} %copy-done.5, f32[2,1024]{1,0:T(2,128)} %copy-done.10, f32[2,640,1024]{2,1,0:T(8,128)} %get-tuple-element.15, f32[3,2,640,1024]{3,2,1,0:T(8,128)} %get-tuple-element.16, f32[]{:T(128)} %bitcast.4), kind=kOutput, calls=%fused_computation.6 | output fusion | flops 17042048 | bytes 34096128 | tf_op jit(solution)/shard_map/mul | solution.py:335
  468.1 1.2 fusion.20
  469.3 2.5 add_bitcast_fusion
  471.8 0.7 copy-done.3
  472.5 13.0 %multiply_convert_fusion.1 = bf16[2,640,1024]{2,1,0:T(8,128)(2,1)S(1)} fusion(f32[1,640,1024]{2,1,0:T(8,128)S(1)} %copy-done.1, f32[1,640,1024]{2,1,0:T(8,128)S(1)} %copy-done.3, f32[2,1024]{1,0:T(2,128)S(1)} %copy-done.8, f32[2,640,1024]{2,1,0:T(8,128)} %get-tuple-element.14, f32[2,640,1024]{2,1,0:T(8,128)} %get-tuple-element.13, ...), kind=kOutput, calls=%fused_computation.9 | output fusion | flops 19663488 | bytes 44581888 | tf_op jit(solution)/shard_map/mul | solution.py:335
  485.5 2.6 fusion.23
  488.2 2.4 add_bitcast_fusion.1
  490.5 0.8 copy-done.9
  491.5 0.6 fusion.31
  494.7 32.1 %psum.21 = f32[3]{0:T(128)S(1)} all-reduce(f32[3]{0:T(128)S(1)} %pad_maximum_fusion.3), channel_id=1, replica_groups=mesh['replica'=2,'data'=8] {'replica','data'}, use_global_device_ids=true, to_apply=%region_3.0 | all-reduce | flops 3 | bytes 24 | tf_op jit(solution)/shard_map/psum | solution.py:357
  526.8 0.6 fusion.30
  527.4 40.2 %all-reduce.3.cloned.1.call-done = (f32[640,640]{0,1:T(8,128)}, f32[768,640]{0,1:T(8,128)}) async-done(((f32[640,640]{0,1:T(8,128)}, f32[768,640]{0,1:T(8,128)}), (f32[640,640]{0,1:T(8,128)}, f32[768,640]{0,1:T(8,128)})) %all-reduce.3.cloned.1.call-update) | async-done | bytes 3604496 | tf_op jit(solution)/shard_map/psum | solution.py:357
  567.5 2.9 copy.12
  570.5 1.7 copy.11
  (37 shorter events, 0.6 us)
Async XLA Ops:
  7.2 3.0 copy-start.13
  7.2 3.0 copy-start.16
  7.2 560.4 %all-reduce.3.cloned.1.call-start = ((), (), s32[]{:S(2)}) async-start(), calls=%async_computation | async-start | bytes 7208960 | tf_op jit(solution)/shard_map/psum | solution.py:357
  10.2 8.1 %copy-start = (f32[1,640,1024]{2,1,0:T(8,128)}, f32[1,640,1024]{2,1,0:T(8,128)S(1)}, u32[]{:S(2)}) copy-start(f32[1,640,1024]{2,1,0:T(8,128)S(1)} %convolution_bitcast_fusion) | copy-start | bytes 7864324
  10.2 2.8 copy-start.11
  10.2 3.1 copy-start.15
  13.3 5.0 copy-start.2
  14.5 3.8 copy-start.4
  15.8 2.6 copy-start.5
  16.4 5.3 copy-start.7
  17.0 4.7 copy-start.10
  455.7 12.3 %copy-start.12 = (bf16[2048,768]{1,0:T(8,128)(2,1)S(1)}, bf16[2048,768]{1,0:T(8,128)(2,1)}, u32[]{:S(2)}) copy-start(bf16[2048,768]{1,0:T(8,128)(2,1)} %param.7) | copy-start | bytes 9437188
  469.3 2.5 copy-start.1
  469.3 3.2 copy-start.3
  469.3 3.2 copy-start.8
  485.5 2.7 copy-start.14
  490.5 0.8 copy-start.9
  567.5 3.0 copy-start.6
Sparse Core Ops, SparseCore 0:
  490.7 76.8 all-reduce.2

commit v3 on v2

--- a/solution.py
+++ b/solution.py
@@ -16,19 +16,23 @@
 LN2 = 0.6931471805599453
 BM, HALF, BN, SN, QR = 1024, 1024, 512, 256, 16
 CHUNKS, PER = 2 * HALF // BN, BN // SN
-IMG_SEQ = (0, 1, 0, 2, 3, 2, 3, 0, 1, 3, 2, 3, 2, 1, 0, 1)
-TXT_SEQ = (0, 1, 1, 1, 1, 2, 2, 2, 2, 3, 3, 0, 0, 3, 3, 0)
-STEPS = 2 * len(IMG_SEQ)
+TAIL = 512
+OUT_ROWS, PART = 1536, 96
+CHUNK_SEQ = (0, 1, 2, 3, 0, 1, 4, 5, 6, 7, 4, 5, 6, 7, 0, 1, 2, 3, 7, 6, 4, 5, 6, 4, 7, 5, 2, 3, 0, 1, 2, 3)
+TXT_SEQ = (0, 0, 1, 1, 1, 1, 1, 1, 1, 1, 2, 2, 2, 2, 2, 2, 2, 2, 3, 3, 3, 3, 0, 0, 0, 0, 3, 3, 3, 3, 0, 0)
+STEPS = len(CHUNK_SEQ)
 
 
 def dot(a, b, dims=NN):
     return lax.dot_general(a, b, dims, preferred_element_type=F32)
 
 
-def entry(seq, u):
-    low, high = (sum(v << (2 * k) for k, v in enumerate(part)) for part in (seq[:8], seq[8:]))
-    code = low + (u // 8) * (high - low)
-    return (code >> (2 * (u % 8))) % 4
+def entry(seq, n):
+    codes = [sum(v << (3 * k) for k, v in enumerate(seq[first:first + 8])) for first in range(0, STEPS, 8)]
+    code = codes[0]
+    for k in range(1, len(codes)):
+        code = code + jnp.minimum(jnp.maximum(n // 8 - k + 1, 0), 1) * (codes[k] - codes[k - 1])
+    return (code >> (3 * (n % 8))) % 8
 
 
 def is_first(n):
@@ -48,6 +52,7 @@
     behind = (rep, 4 * (1 - x) + 2 * y + core)
     twin = (rep, 4 * y + 2 * x + (1 - core))
     far = (1 - rep, dat)
+    across = (rep, 4 * (1 - y) + 2 * (1 - x) + core)
     scale, shift = sc_ref[0], sc_ref[1]
 
     def remote(src, dst, sems, k, to):
@@ -62,7 +67,7 @@
         return remote(src, it_all.at[2 + 2 * kind + c], (i_send, i_recv), 2 * kind + c, (twin, far, twin)[kind])
 
     def dt_hop(s, h):
-        return remote(acc.at[(1, 2, 1)[s], h], inc_t.at[s, h], (dt_send, dt_recv), 2 * s + h, (ahead, behind)[h])
+        return remote(acc.at[(1, 2, 1)[s], h], inc_t.at[s, h], (dt_send, dt_recv), 2 * s + h, ((behind, ahead), (across, across), (ahead, behind))[s][h])
 
     def di_hop(kind, c):
         src = di_ref.at[(6, 4, 2)[kind] + c]
@@ -76,8 +81,18 @@
                 cp.start()
             for p, cp in enumerate(copies):
                 cp.wait()
-                cols = pl.ds(first + p * SN, SN)
-                dst[:, cols] += s_buf[p, 0:rows, :]
+
+                def add_rows(i, _):
+                    part = pl.ds(i * 64, 64)
+                    dst[part, pl.ds(first + p * SN, SN)] += s_buf[p, part, :]
+
+                lax.fori_loop(0, rows // 64, add_rows, None)
+
+    def clear(dst):
+        def clear_rows(i, _):
+            dst[pl.ds(i * 64, 64), :] = jnp.zeros((64, dst.shape[1]), F32)
+
+        lax.fori_loop(0, dst.shape[0] // 64, clear_rows, None)
 
     def load(chunk, slot):
         return pltpu.make_async_copy(di_ref.at[chunk], slots.at[slot], load_sem.at[slot])
@@ -86,12 +101,12 @@
         return pltpu.make_async_copy(slots.at[slot], di_ref.at[chunk], store_sem.at[slot])
 
     def chunk_of(n):
-        return 2 * entry(IMG_SEQ, n // 2) + n % 2
+        return entry(CHUNK_SEQ, n)
 
     barrier = pltpu.get_barrier_semaphore()
-    for to in (ahead, behind, twin, far):
+    for to in (ahead, behind, across, twin, far):
         pl.semaphore_signal(barrier, inc=1, device_id=to, device_id_type=MESH)
-    pl.semaphore_wait(barrier, 4)
+    pl.semaphore_wait(barrier, 5)
 
     own = [pltpu.make_async_copy(img_ref.at[c], it_all.at[c], init_sem.at[c]) for c in range(2)]
     own += [pltpu.make_async_copy(txt_ref.at[h], t_all.at[0, h], init_sem.at[2 + h]) for h in range(2)]
@@ -107,91 +122,101 @@
     for cp in own:
         cp.wait()
 
+    def arrivals(n):
+        @pl.when(n == 2)
+        def _():
+            img_hop(0, 0).wait_recv()
+            for h in range(2):
+                txt_hop(1, h).wait_recv()
+                txt_hop(2, h).start()
+
+        @pl.when(n == 3)
+        def _():
+            img_hop(0, 1).wait_recv()
+
+        @pl.when(n == 5)
+        def _():
+            img_hop(1, 0).wait_recv()
+            img_hop(2, 0).start()
+
+        @pl.when(n == 6)
+        def _():
+            for h in range(2):
+                txt_hop(2, h).wait_recv()
+                txt_hop(3, h).start()
+
+        @pl.when(n == 7)
+        def _():
+            img_hop(1, 1).wait_recv()
+            img_hop(2, 1).start()
+
+        @pl.when(n == 8)
+        def _():
+            img_hop(2, 0).wait_recv()
+
+        @pl.when(n == 9)
+        def _():
+            img_hop(2, 1).wait_recv()
+
+        @pl.when(n == 10)
+        def _():
+            for h in range(2):
+                dt_hop(0, h).start()
+
+        @pl.when(n == 18)
+        def _():
+            for h in range(2):
+                dt_hop(1, h).start()
+            for h in range(2):
+                dt_hop(0, h).wait_send()
+                txt_hop(3, h).wait_recv()
+
+        @pl.when(n == 30)
+        def _():
+            for h in range(2):
+                dt_hop(2, h).start()
+
     def step(n, diag):
-        tb = entry(TXT_SEQ, n // 2)
+        tb = entry(TXT_SEQ, n)
         ab = tb - 2 * (tb // 3)
         chunk, slot, after = chunk_of(n), n % 3, (n + 1) % 3
 
-        if not diag:
-            @pl.when(n == 2)
-            def _():
-                img_hop(0, 0).wait_recv()
-                for h in range(2):
-                    txt_hop(1, h).wait_recv()
-                    txt_hop(2, h).start()
-
-            @pl.when(n == 3)
-            def _():
-                img_hop(0, 1).wait_recv()
-
-            @pl.when(n == 5)
-            def _():
-                img_hop(1, 0).wait_recv()
-                img_hop(2, 0).start()
-
-            @pl.when(n == 6)
+        @pl.when((n < 11) | (n == 18) | (n == 30))
+        def _():
+            if not diag:
+                arrivals(n)
+
+            @pl.when((n == 0) | (n == 2) | (n == 10) | (n == 18))
             def _():
                 for h in range(2):
-                    txt_hop(2, h).wait_recv()
-                    txt_hop(3, h).start()
-
-            @pl.when(n == 7)
+                    clear(acc.at[ab, h])
+
+            @pl.when(is_first(n))
             def _():
-                img_hop(1, 1).wait_recv()
-                img_hop(2, 1).start()
-
-            @pl.when(n == 8)
+                def turn(i, _):
+                    part = pl.ds(pl.multiple_of(i * 256, 256), 256)
+                    i_all[chunk, part, :] = it_all[chunk, :, part].T
+
+                lax.fori_loop(0, BM // 256, turn, None)
+                clear(slots.at[slot])
+
+        @pl.when(jnp.logical_not(is_first(n)))
+        def _():
+            load(chunk, slot).wait()
+
+        @pl.when((n >= 2) & (n != 24) & (n != 25) & (n != 26) & (n != 27))
+        def _():
+            store(chunk_of(n - 2), after).wait()
+
+        @pl.when((n < STEPS - 1) & jnp.logical_not(is_first(n + 1)))
+        def _():
+            load(chunk_of(n + 1), after).start()
+
+        if not diag:
+            @pl.when((n == 23) | (n == 25))
             def _():
-                img_hop(2, 0).wait_recv()
-
-            @pl.when(n == 9)
-            def _():
-                img_hop(2, 1).wait_recv()
-
-            @pl.when(n == 10)
-            def _():
-                for h in range(2):
-                    dt_hop(0, h).start()
-
-            @pl.when(n == 18)
-            def _():
-                for h in range(2):
-                    dt_hop(1, h).start()
-                for h in range(2):
-                    dt_hop(0, h).wait_send()
-                    txt_hop(3, h).wait_recv()
-
-            @pl.when(n == 30)
-            def _():
-                for h in range(2):
-                    dt_hop(2, h).start()
-
-        @pl.when((n == 0) | (n == 2) | (n == 10) | (n == 18))
-        def _():
-            acc[ab] = jnp.zeros(acc.shape[1:], F32)
-
-        @pl.when(is_first(n))
-        def _():
-            i_all[chunk] = it_all[chunk].T
-            slots[slot] = jnp.zeros(slots.shape[1:], F32)
-
-        @pl.when(jnp.logical_not(is_first(n)))
-        def _():
-            load(chunk, slot).wait()
-
-        @pl.when((n >= 2) & (n != 26) & (n != 27))
-        def _():
-            store(chunk_of(n - 2), after).wait()
-
-        @pl.when((n < STEPS - 1) & jnp.logical_not(is_first(n + 1)))
-        def _():
-            load(chunk_of(n + 1), after).start()
-
-        if not diag:
-            for c in range(2):
-                @pl.when(n == 24 + c)
-                def _():
-                    di_hop(0, c).start()
+                store(chunk_of(n - 1), (n - 1) % 3).wait()
+                di_hop(0, (n - 23) // 2).start()
 
         def similarity(k):
             h, cols = (k * SN) // HALF, pl.ds((k * SN) % HALF, SN)
@@ -239,29 +264,17 @@
                 gradients((k - 1) // PER - 1)
 
         if not diag:
-            @pl.when(n == 17)
+            @pl.when((n == 23) | (n == 25))
             def _():
-                for h in range(2):
-                    dt_hop(0, h).wait_recv()
-                    add_from(acc.at[2, h], inc_t.at[0, h])
-
-            @pl.when(n == 29)
-            def _():
-                for h in range(2):
-                    dt_hop(1, h).wait_recv()
-                    add_from(acc.at[1, h], inc_t.at[1, h])
-
-            for c in range(2):
-                @pl.when(n == 24 + c)
-                def _():
-                    di_hop(0, c).wait_recv()
-                    add_from(slots.at[c], inc_core.at[c])
-                    to_hbm = pltpu.make_async_copy(slots.at[c], di_ref.at[4 + c], far_sem.at[c])
-                    to_hbm.start()
-                    to_hbm.wait()
-                    di_hop(1, c).start()
-
-        @pl.when((n != 24) & (n != 25))
+                c = (n - 23) // 2
+                di_hop(0, c).wait_recv()
+                add_from(slots.at[slot], inc_core.at[c])
+                to_hbm = pltpu.make_async_copy(slots.at[slot], di_ref.at[4 + c], far_sem.at[c])
+                to_hbm.start()
+                to_hbm.wait()
+                di_hop(1, c).start()
+
+        @pl.when((n != 23) & (n != 25))
         def _():
             store(chunk, slot).start()
 
@@ -288,8 +301,9 @@
             di_hop(kind, c).wait_send()
     for cp in final:
         cp.wait()
-    for h in range(2):
-        dt_hop(2, h).wait_recv()
+    for s in range(3):
+        for h in range(2):
+            dt_hop(s, h).wait_recv()
     for kind in (1, 2):
         for c in range(2):
             di_hop(kind, c).wait_recv()
@@ -328,13 +342,170 @@
     halves = [lax.dot_general(w, x[k * HALF:(k + 1) * HALF], (((0,), (1,)), ((), ())), preferred_element_type=F32) for k in range(2)]
     raw = jnp.stack(halves)
     inv = lax.rsqrt(jnp.sum(raw * raw, axis=1, keepdims=True))
-    return raw * inv, inv
-
-
-def weight_grad(x, unit, inv, grad):
-    raw_grad = (inv * (grad - unit * jnp.sum(unit * grad, axis=1, keepdims=True))).astype(BF16)
-    parts = [lax.dot_general(x[k * HALF:(k + 1) * HALF], raw_grad[k], (((0,), (1,)), ((), ())), preferred_element_type=F32) for k in range(2)]
-    return parts[0] + parts[1]
+    return raw, (raw * inv).astype(BF16)
+
+
+def tail_kernel(img_sc, txt_sc, st_ref, *refs):
+    *ins, out_ref, img_acc, txt_acc = refs
+    sums, raws, xs = ins[:3], ins[3], ins[4]
+    txt_sums, txt_raw, txt_x = ins[5:9], ins[9], ins[10]
+    g = pl.program_id(0)
+    dim, img_rows = out_ref.shape[1], xs.shape[1]
+
+    def add_rows(factor, parts, raw_ref, x_ref, acc, start):
+        total = parts[0][...].reshape(dim, TAIL)
+        for part in parts[1:]:
+            total = total + part[...].reshape(dim, TAIL)
+        grad = factor[0] * total
+        raw = raw_ref[0]
+        inv = lax.rsqrt(jnp.sum(raw * raw, axis=0, keepdims=True))
+        unit = raw * inv
+        raw_grad = inv * (grad - unit * jnp.sum(unit * grad, axis=0, keepdims=True))
+        part = dot(raw_grad.astype(BF16), x_ref[...])
+
+        @pl.when(g == start)
+        def _():
+            acc[...] = part
+
+        @pl.when(g > start)
+        def _():
+            acc[...] += part
+
+    @pl.when(g < 4)
+    def _():
+        add_rows(img_sc, sums, raws, xs, img_acc, 0)
+
+    @pl.when(g >= 4)
+    def _():
+        add_rows(txt_sc, txt_sums, txt_raw, txt_x, txt_acc, 4)
+
+    @pl.when(g == 4)
+    def _():
+        out_ref[0:img_rows, :] = img_acc[...].T
+
+    @pl.when(g == 7)
+    def _():
+        last = img_rows + txt_acc.shape[1]
+        out_ref[img_rows:last, :] = txt_acc[...].T
+        total_rows = txt_sc[1]
+        loss = (jnp.sum(st_ref[0]) * LN2 + jnp.sum(st_ref[1])) / total_rows
+        d_temp = txt_sc[0] * jnp.sum(st_ref[3])
+        d_bias = jnp.sum(st_ref[2]) / total_rows
+        row = lax.broadcasted_iota(jnp.int32, (OUT_ROWS - last, dim), 0)
+        out_ref[last:OUT_ROWS, :] = jnp.where(row == 0, loss, jnp.where(row == 1, d_temp, d_bias))
+
+
+def tail(sc, st, di, inc_own, inc_z, img_raw, img_x, dt0, inc_t, txt_raw, txt_x):
+    dim = img_raw.shape[1]
+    img_f, txt_f = img_x.shape[1], txt_x.shape[1]
+    img_g = lambda g: jnp.minimum(g, 3)
+    txt_g = lambda g: jnp.maximum(g - 4, 0)
+    block = lambda at: pl.BlockSpec((1, dim, TAIL), lambda g: (at(g) // 2, 0, at(g) % 2))
+    rows = lambda at, f: pl.BlockSpec((TAIL, f), lambda g: (at(g), 0))
+    hop = lambda s: pl.BlockSpec((1, 1, dim, TAIL), lambda g: (s, txt_g(g) // 2, 0, txt_g(g) % 2))
+    smem = pl.BlockSpec(memory_space=pltpu.SMEM)
+    out_rows = OUT_ROWS
+    return pl.pallas_call(
+        tail_kernel,
+        name="tail",
+        grid=(8,),
+        out_shape=jax.ShapeDtypeStruct((out_rows, dim), F32),
+        in_specs=[smem, smem, pl.BlockSpec(st.shape, lambda g: (0, 0, 0)), block(img_g), block(img_g), block(img_g), block(img_g), rows(img_g, img_f),
+                  block(txt_g), hop(0), hop(1), hop(2), block(txt_g), rows(txt_g, txt_f)],
+        out_specs=pl.BlockSpec((out_rows, dim), lambda g: (0, 0)),
+        scratch_shapes=[pltpu.VMEM((dim, img_f), F32), pltpu.VMEM((dim, txt_f), F32)],
+        compiler_params=pltpu.CompilerParams(vmem_limit_bytes=60 * 2**20, dimension_semantics=("arbitrary",)),
+    )(sc, sc, st, di, inc_own, inc_z, img_raw, img_x, dt0, inc_t, inc_t, inc_t, txt_raw, txt_x)
+
+
+def reduce_kernel(x_ref, img_ref, txt_ref, tot_ref, from_twin, part, got, res, t_send, t_recv, p_send, p_recv, g_send, g_recv, f_send, f_recv, out_sem):
+    rep, dat = lax.axis_index("replica"), lax.axis_index("data")
+    y, x, core = dat // 4, (dat // 2) % 2, dat % 2
+
+    def flip(bit, on):
+        return 1 - bit if on else bit
+
+    def chip(q):
+        return flip(rep, q & 4), flip(y, q & 2), flip(x, q & 1)
+
+    def device(q):
+        cz, cy, cx = chip(q)
+        return (cz, 4 * cy + 2 * cx + core)
+
+    def rows(c, k):
+        return pl.ds((2 * c + k) * PART, PART)
+
+    def number(q):
+        cz, cy, cx = chip(q)
+        return 4 * cz + 2 * cy + cx
+
+    twin = (rep, 4 * y + 2 * x + (1 - core))
+
+    def remote(src, dst, sems, k, to):
+        return pltpu.make_async_remote_copy(src_ref=src, dst_ref=dst, send_sem=sems[0].at[k], recv_sem=sems[1].at[k], device_id=to, device_id_type=MESH)
+
+    barrier = pltpu.get_barrier_semaphore()
+    for to in [twin] + [device(q) for q in range(1, 8)]:
+        pl.semaphore_signal(barrier, inc=1, device_id=to, device_id_type=MESH)
+    pl.semaphore_wait(barrier, 8)
+
+    halves = [remote(x_ref.at[rows(c, 1 - core)], from_twin.at[c], (t_send, t_recv), c, twin) for c in range(8)]
+    for cp in halves:
+        cp.start()
+    for c, cp in enumerate(halves):
+        cp.wait_recv()
+        part[c] = x_ref[rows(c, core), :] + from_twin[c]
+    parts = [remote(part.at[number(q)], got.at[q - 1], (p_send, p_recv), q - 1, device(q)) for q in range(1, 8)]
+    for cp in parts:
+        cp.start()
+    total = part[number(0)]
+    for q, cp in enumerate(parts):
+        cp.wait_recv()
+        total = total + got[q]
+    mine = rows(number(0), core)
+    res[mine, :] = total
+    spread = [remote(res.at[mine], res.at[mine], (g_send, g_recv), q - 1, device(q)) for q in range(1, 8)]
+    for cp in spread:
+        cp.start()
+    forward = [remote(res.at[rows(number(q), core)], res.at[rows(number(q), core)], (f_send, f_recv), q, twin) for q in range(8)]
+    forward[0].start()
+    for q in range(1, 8):
+        arrived = res.at[rows(number(q), core)]
+        remote(arrived, arrived, (g_send, g_recv), q - 1, device(q)).wait_recv()
+        forward[q].start()
+    for q in range(8):
+        other = res.at[rows(number(q), 1 - core)]
+        remote(other, other, (f_send, f_recv), q, twin).wait_recv()
+    first, last = img_ref.shape[0], img_ref.shape[0] + txt_ref.shape[0]
+    spans = ((img_ref, 0, first), (txt_ref, first, last), (tot_ref, last, last + 8))
+    outs = [pltpu.make_async_copy(res.at[pl.ds(lo, hi - lo)], ref, out_sem.at[k]) for k, (ref, lo, hi) in enumerate(spans)]
+    for cp in outs:
+        cp.start()
+    for cp in halves + parts + spread + forward:
+        cp.wait_send()
+    for cp in outs:
+        cp.wait()
+
+
+def reduce_all(x, img_f, txt_f):
+    dim = x.shape[1]
+    any_spec = pl.BlockSpec(memory_space=pl.ANY)
+    dma = lambda k: pltpu.SemaphoreType.DMA((k,))
+    return pl.pallas_call(
+        reduce_kernel,
+        name="reduce",
+        out_shape=tuple(jax.ShapeDtypeStruct((k, dim), F32) for k in (img_f, txt_f, 8)),
+        in_specs=[pl.BlockSpec(memory_space=pltpu.VMEM)],
+        out_specs=(any_spec,) * 3,
+        scratch_shapes=[
+            pltpu.VMEM((8, PART, dim), F32),
+            pltpu.VMEM((8, PART, dim), F32),
+            pltpu.VMEM((7, PART, dim), F32),
+            pltpu.VMEM((OUT_ROWS, dim), F32),
+            dma(8), dma(8), dma(7), dma(7), dma(7), dma(7), dma(8), dma(8), dma(3),
+        ],
+        compiler_params=pltpu.CompilerParams(vmem_limit_bytes=40 * 2**20, collective_id=1, has_side_effects=True),
+    )(x)
 
 
 def solution(mesh):
@@ -343,19 +514,15 @@
 
     def local_fn(img_x, txt_x, w_img, w_txt, log_temp, logit_bias):
         total_rows = img_x.shape[0] * dev_count
-        img_unit, img_inv = embed_t(img_x, w_img)
-        txt_unit, txt_inv = embed_t(txt_x, w_txt)
+        img_raw, img_t = embed_t(img_x, w_img)
+        txt_raw, txt_t = embed_t(txt_x, w_txt)
         temp_scale = jnp.exp(log_temp[0])
         sc = jnp.stack([temp_scale * LOG2E, logit_bias[0] * LOG2E])
-        st, di, dt0, inc_t, _, inc_z, inc_own = score(sc, img_unit.astype(BF16), txt_unit.astype(BF16))
-        scale = temp_scale / total_rows
-        d_w_txt = weight_grad(txt_x, txt_unit, txt_inv, scale * (dt0 + inc_t[2]))
-        d_w_img = weight_grad(img_x, img_unit, img_inv, scale * (di[0:2] + inc_own + inc_z))
-        sums = jnp.sum(st, axis=(1, 2))
-        loss_sum = sums[0] * LN2 + sums[1]
-        totals = jnp.stack([loss_sum / total_rows, temp_scale * sums[3] / total_rows, sums[2] / total_rows])
-        totals, d_w_txt, d_w_img = lax.psum((totals, d_w_txt, d_w_img), batch_axes)
-        return totals[0:1], totals[1:2], totals[2:3], d_w_img, d_w_txt
+        st, di, dt0, inc_t, _, inc_z, inc_own = score(sc, img_t, txt_t)
+        factors = jnp.stack([temp_scale / total_rows, jnp.float32(total_rows)])
+        grads = tail(factors, st, di, inc_own, inc_z, img_raw, img_x, dt0, inc_t, txt_raw, txt_x)
+        d_w_img, d_w_txt, totals = reduce_all(grads, img_x.shape[1], txt_x.shape[1])
+        return totals[0, 0:1], totals[1, 0:1], totals[2, 0:1], d_w_img, d_w_txt
 
     batch_spec = P(batch_axes, None)
     return jax.shard_map(local_fn, mesh=mesh, in_specs=(batch_spec, batch_spec, P(), P(), P(), P()), out_specs=(P(), P(), P(), P(), P()), check_vma=False)

time: 585 us -> 541 us (0.925)
  Pallas kernels: 434 us -> 515 us
  waiting for transfers between devices: 40.2 us -> 0 us
  blocking collectives: 32.1 us -> 0 us
  other arithmetic: 30.4 us -> 11.1 us
  between operations: 18.7 us -> 2.05 us
  matrix products: 15.3 us -> 6.63 us
    pallas_call x0 -> x2, Pallas kernels: none -> 88.4 us  [the longest x1 62.8 us: reduce_all(): pl.pallas_call(reduce_kernel, name='reduce', out_shape=tuple((jax.ShapeDt...]
    psum x1 -> x0, waiting for transfers between devices: 40.2 us -> none  [local_fn(): totals, d_w_txt, d_w_img = lax.psum((totals, d_w_txt, d_w_img), batch_axes)]
    psum x1 -> x0, blocking collectives: 32.1 us -> none  [local_fn(): totals, d_w_txt, d_w_img = lax.psum((totals, d_w_txt, d_w_img), batch_axes)]
    mul x2 -> x0, other arithmetic: 25.3 us -> none  [weight_grad(): unit * jnp.sum(unit * grad, axis=1, keepdims=True)]
    dot_general x4 -> x0, matrix products: 8.69 us -> none  [weight_grad(): lax.dot_general(x[k * HALF:(k + 1) * HALF], raw_grad[k], (((0,), (1,)), (...]
    pallas_call x1, Pallas kernels: 434 us -> 426 us  [score(): pl.pallas_call(kernel, name='score', out_shape=(jax.ShapeDtypeStruct((4,...]
    another operation x1 -> x3, other arithmetic: 0.08 us -> 7 us  [the longest x2 6.42 us: embed_t(): raw = jnp.stack(halves)]
  transfers between devices with their start and end apart: 1 -> 0, of which waited for: 1 -> 0; matrix products, arithmetic and copies ran while one was open for 0% -> 0% of each run, Pallas kernels for 0% -> 0%
where the time goes in v3:
time: 541 us; the launch traced here: 540 us
  Pallas kernels  515 us (95%)
  other arithmetic  11.1 us (2%)
  matrix products  6.63 us (1%)
  local copies, waits for them, and re-layouts  6 us (1%)
    pallas_call x1, Pallas kernels, score(): pl.pallas_call(kernel, name='score', out_shape=(jax.ShapeDtypeStruct((4,...  426 us
    pallas_call x1, Pallas kernels, reduce_all(): pl.pallas_call(reduce_kernel, name='reduce', out_shape=tuple((jax.ShapeDt...  62.8 us
    pallas_call x1, Pallas kernels, tail(): pl.pallas_call(tail_kernel, name='tail', grid=(8,), out_shape=jax.ShapeDt...  25.6 us

profile of v3, /device:TPU:0, one launch (start us, length us, event | category | flops | bytes accessed | tf_op | source)
XLA Modules:
  0.0 540.5 jit_solution(16024848868329631494)
XLA Ops:
  2.0 0.6 pad_maximum_fusion.3.sc_ref
  2.6 0.6 pad_maximum_fusion.2.img_sc.txt_sc
  3.1 0.0 copy-start.2
  3.1 0.0 copy-start.4
  3.1 2.9 convolution_bitcast_fusion
  6.1 0.0 copy-done.2
  6.1 0.0 copy-done.4
  6.1 0.0 copy-start.1
  6.1 0.0 copy-start.3
  6.1 1.2 convolution_bitcast_fusion.1
  7.4 0.6 copy-done.1
  8.0 0.3 copy-done.3
  8.3 1.2 convolution_bitcast_fusion.2
  9.5 1.2 convolution_bitcast_fusion.3
  10.7 3.2 pad_maximum_fusion.1
  13.9 3.2 pad_maximum_fusion
  17.2 3.5 multiply_convert_fusion
  20.7 426.3 %score.1 = (f32[4,16,256]{2,1,0:T(8,128)}, f32[8,640,1024]{2,1,0:T(8,128)}, f32[2,640,1024]{2,1,0:T(8,128)}, f32[3,2,640,1024]{3,2,1,0:T(8,128)}, f32[2,640,1024...) custom-call(f32[2]{0:T(128)} %pad_maximum_fusion.3.sc_ref, ...), custom_call_target="tpu_custom_call" | custom-call | flops 257698037760 | bytes 268435456 | tf_op jit(solution)/shard_map/score/pallas_call | solution.py:319
  446.9 25.6 %tail.1.x_ref = f32[1536,640]{1,0:T(8,128)} custom-call(f32[2]{0:T(128)} %pad_maximum_fusion.2.img_sc.txt_sc, f32[2]{0:T(128)} %pad_maximum_fusion.2.img_sc.txt_sc, f32[4,16,256]{2,1,0:T(8,128)} %get-tuple-element.14.st_ref, f32[8,640,1024]{2,1,0:T(8,128)} %get-tuple-element.15.refs_0_, f32[2,640,1024]{2,1,0:T(8,128)} %get-tuple-element.16.refs_1_, ...), custom_call_target="tpu_custom_call" | custom-call | tf_op jit(solution)/shard_map/tail/pallas_call | solution.py:408
  472.6 2.1 copy-done
  474.7 62.8 %reduce.1 = (f32[640,640]{1,0:T(8,128)S(1)}, f32[768,640]{1,0:T(8,128)S(1)}, f32[8,640]{1,0:T(8,128)S(1)}) custom-call(f32[1536,640]{1,0:T(8,128)S(1)} %copy-done), custom_call_target="tpu_custom_call" | custom-call | tf_op jit(solution)/shard_map/reduce/pallas_call | solution.py:494
  537.5 0.5 fusion.4
  538.0 1.2 copy.15
  539.2 1.3 copy.16
  (3 shorter events, 0.0 us)
Async XLA Ops:
  3.1 3.0 copy-start.2
  3.1 3.0 copy-start.4
  6.1 1.9 copy-start.1
  6.1 2.1 copy-start.3
  472.6 2.1 copy-start

commit v4 on v3

--- a/solution.py
+++ b/solution.py
@@ -59,11 +59,11 @@
         return pltpu.make_async_remote_copy(src_ref=src, dst_ref=dst, send_sem=sems[0].at[k], recv_sem=sems[1].at[k], device_id=to, device_id_type=MESH)
 
     def txt_hop(s, h):
-        src = txt_ref.at[h] if s == 1 else t_all.at[s - 1, h]
+        src = txt_ref.at[:, pl.ds(h * HALF, HALF)] if s == 1 else t_all.at[s - 1, h]
         return remote(src, t_all.at[s, h], (t_send, t_recv), 2 * (s - 1) + h, (ahead, behind)[h])
 
     def img_hop(kind, c):
-        src = it_all.at[4 + c] if kind == 2 else img_ref.at[c]
+        src = it_all.at[4 + c] if kind == 2 else img_ref.at[:, pl.ds(c * BM, BM)]
         return remote(src, it_all.at[2 + 2 * kind + c], (i_send, i_recv), 2 * kind + c, (twin, far, twin)[kind])
 
     def dt_hop(s, h):
@@ -108,8 +108,8 @@
         pl.semaphore_signal(barrier, inc=1, device_id=to, device_id_type=MESH)
     pl.semaphore_wait(barrier, 5)
 
-    own = [pltpu.make_async_copy(img_ref.at[c], it_all.at[c], init_sem.at[c]) for c in range(2)]
-    own += [pltpu.make_async_copy(txt_ref.at[h], t_all.at[0, h], init_sem.at[2 + h]) for h in range(2)]
+    own = [pltpu.make_async_copy(img_ref.at[:, pl.ds(c * BM, BM)], it_all.at[c], init_sem.at[c]) for c in range(2)]
+    own += [pltpu.make_async_copy(txt_ref.at[:, pl.ds(h * HALF, HALF)], t_all.at[0, h], init_sem.at[2 + h]) for h in range(2)]
     for cp in own:
         cp.start()
     for h in range(2):
@@ -310,7 +310,7 @@
 
 
 def score(sc, img_t, txt_t):
-    dim = img_t.shape[1]
+    dim = img_t.shape[0]
     any_spec = pl.BlockSpec(memory_space=pl.ANY)
     piece = (dim, HALF)
     hbm = lambda *lead: jax.ShapeDtypeStruct((*lead, *piece), F32)
@@ -339,9 +339,8 @@
 
 
 def embed_t(x, w):
-    halves = [lax.dot_general(w, x[k * HALF:(k + 1) * HALF], (((0,), (1,)), ((), ())), preferred_element_type=F32) for k in range(2)]
-    raw = jnp.stack(halves)
-    inv = lax.rsqrt(jnp.sum(raw * raw, axis=1, keepdims=True))
+    raw = lax.dot_general(w, x, (((0,), (1,)), ((), ())), preferred_element_type=F32)
+    inv = lax.rsqrt(jnp.sum(raw * raw, axis=0, keepdims=True))
     return raw, (raw * inv).astype(BF16)
 
 
@@ -357,7 +356,7 @@
         for part in parts[1:]:
             total = total + part[...].reshape(dim, TAIL)
         grad = factor[0] * total
-        raw = raw_ref[0]
+        raw = raw_ref[...]
         inv = lax.rsqrt(jnp.sum(raw * raw, axis=0, keepdims=True))
         unit = raw * inv
         raw_grad = inv * (grad - unit * jnp.sum(unit * grad, axis=0, keepdims=True))
@@ -396,11 +395,12 @@
 
 
 def tail(sc, st, di, inc_own, inc_z, img_raw, img_x, dt0, inc_t, txt_raw, txt_x):
-    dim = img_raw.shape[1]
+    dim = img_raw.shape[0]
     img_f, txt_f = img_x.shape[1], txt_x.shape[1]
     img_g = lambda g: jnp.minimum(g, 3)
     txt_g = lambda g: jnp.maximum(g - 4, 0)
     block = lambda at: pl.BlockSpec((1, dim, TAIL), lambda g: (at(g) // 2, 0, at(g) % 2))
+    flat = lambda at: pl.BlockSpec((dim, TAIL), lambda g: (0, at(g)))
     rows = lambda at, f: pl.BlockSpec((TAIL, f), lambda g: (at(g), 0))
     hop = lambda s: pl.BlockSpec((1, 1, dim, TAIL), lambda g: (s, txt_g(g) // 2, 0, txt_g(g) % 2))
     smem = pl.BlockSpec(memory_space=pltpu.SMEM)
@@ -410,8 +410,8 @@
         name="tail",
         grid=(8,),
         out_shape=jax.ShapeDtypeStruct((out_rows, dim), F32),
-        in_specs=[smem, smem, pl.BlockSpec(st.shape, lambda g: (0, 0, 0)), block(img_g), block(img_g), block(img_g), block(img_g), rows(img_g, img_f),
-                  block(txt_g), hop(0), hop(1), hop(2), block(txt_g), rows(txt_g, txt_f)],
+        in_specs=[smem, smem, pl.BlockSpec(st.shape, lambda g: (0, 0, 0)), block(img_g), block(img_g), block(img_g), flat(img_g), rows(img_g, img_f),
+                  block(txt_g), hop(0), hop(1), hop(2), flat(txt_g), rows(txt_g, txt_f)],
         out_specs=pl.BlockSpec((out_rows, dim), lambda g: (0, 0)),
         scratch_shapes=[pltpu.VMEM((dim, img_f), F32), pltpu.VMEM((dim, txt_f), F32)],
         compiler_params=pltpu.CompilerParams(vmem_limit_bytes=60 * 2**20, dimension_semantics=("arbitrary",)),

time: 541 us -> 534 us (0.987)
  other arithmetic: 11.1 us -> 5.19 us
    another operation x2 -> x0, other arithmetic: 6.42 us -> none  [embed_t(): raw = jnp.stack(halves)]
where the time goes in v4:
time: 534 us
  Pallas kernels  515 us (96%)
  matrix products  6.7 us (1%)
    pallas_call x1, Pallas kernels, score(): pl.pallas_call(kernel, name='score', out_shape=(jax.ShapeDtypeStruct((4,...  426 us
    pallas_call x1, Pallas kernels, reduce_all(): pl.pallas_call(reduce_kernel, name='reduce', out_shape=tuple((jax.ShapeDt...  62.7 us
    pallas_call x1, Pallas kernels, tail(): pl.pallas_call(tail_kernel, name='tail', grid=(8,), out_shape=jax.ShapeDt...  25.5 us

profile of v4, /device:TPU:0, one launch (start us, length us, event | category | flops | bytes accessed | tf_op | source)
XLA Modules:
  0.0 533.6 jit_solution(12445694787995247631)
XLA Ops:
  2.0 0.6 pad_maximum_fusion.1.sc_ref
  2.6 0.6 pad_maximum_fusion.img_sc.txt_sc
  3.1 0.0 copy-start.3
  3.1 0.0 copy-start.4
  3.1 4.4 multiply_reduce_fusion.1
  7.5 0.0 copy-start.1
  7.6 0.0 copy-done.3
  7.6 0.0 copy-done.4
  7.6 2.3 multiply_reduce_fusion
  9.9 0.0 copy-start.2
  9.9 0.0 copy-done.1
  9.9 4.0 multiply_convert_fusion
  14.0 0.0 copy-done.2
  14.0 426.3 %score.1 = (f32[4,16,256]{2,1,0:T(8,128)}, f32[8,640,1024]{2,1,0:T(8,128)}, f32[2,640,1024]{2,1,0:T(8,128)}, f32[3,2,640,1024]{3,2,1,0:T(8,128)}, f32[2,640,1024...) custom-call(f32[2]{0:T(128)} %pad_maximum_fusion.1.sc_ref, ...), custom_call_target="tpu_custom_call" | custom-call | flops 257698037760 | bytes 268435456 | tf_op jit(solution)/shard_map/score/pallas_call | solution.py:319
  440.3 25.5 %tail.1.x_ref = f32[1536,640]{1,0:T(8,128)} custom-call(f32[2]{0:T(128)} %pad_maximum_fusion.img_sc.txt_sc, f32[2]{0:T(128)} %pad_maximum_fusion.img_sc.txt_sc, f32[4,16,256]{2,1,0:T(8,128)} %get-tuple-element.14.st_ref, f32[8,640,1024]{2,1,0:T(8,128)} %get-tuple-element.15.refs_0_, f32[2,640,1024]{2,1,0:T(8,128)} %get-tuple-element.16.refs_1_, ...), custom_call_target="tpu_custom_call" | custom-call | tf_op jit(solution)/shard_map/tail/pallas_call | solution.py:408
  465.8 0.0 copy-start
  465.8 2.1 copy-done
  467.9 62.7 %reduce.1 = (f32[640,640]{1,0:T(8,128)S(1)}, f32[768,640]{1,0:T(8,128)S(1)}, f32[8,640]{1,0:T(8,128)S(1)}) custom-call(f32[1536,640]{1,0:T(8,128)S(1)} %copy-done), custom_call_target="tpu_custom_call" | custom-call | tf_op jit(solution)/shard_map/reduce/pallas_call | solution.py:494
  530.6 0.5 fusion
  531.2 1.2 copy.15
  532.3 1.3 copy.16
  (2 shorter events, 0.0 us)
Async XLA Ops:
  3.1 4.4 copy-start.3
  3.1 4.4 copy-start.4
  7.5 2.4 copy-start.1
  9.9 4.1 copy-start.2
  465.8 2.1 copy-start
